TPU v7x, 128 devices: a whole 4x4x4 slice. The times are simulated.
128 devices in a mesh: dp: 1, tp: 16 (over z, y), cp: 8 (over x, core).
Axes of the slice: x: 4, y: 4, z: 4, core: 2. Of those that a mesh axis runs over, the one named last changes fastest.
Arguments:
- x: bfloat16 [4096, 8192], P(('dp', 'cp'))
- doc_ids: int32 [4096], P(('dp', 'cp'))
- w_query: bfloat16 [8192, 8192], P(None, 'tp')
- w_key: bfloat16 [8192, 8192], P(None, 'tp')
- w_value: bfloat16 [8192, 8192], P(None, 'tp')
- w_out: bfloat16 [8192, 8192], P('tp')
Outputs:
- output: bfloat16 [4096, 8192], P(('dp', 'cp'))
All inputs are finite; a program needn't handle non-finite values.
Results may differ from a plain program's by a relative error of at most 0.0071832.
Values are sent between devices in bfloat16 or wider.
A program may use at most 1 GiB of HBM per device.

v0:
```python
import jax
import jax.numpy as jnp
from jax import lax
from jax.sharding import PartitionSpec as P

HEAD_DIM = 128


def block_update(soft_state, q_blk, k_blk, v_blk, allowed):
    run_max, run_sum, out_acc = soft_state
    scores = jnp.einsum('qhgd,khd->qhgk', q_blk, k_blk, preferred_element_type=jnp.float32) * (HEAD_DIM ** -0.5)
    scores = jnp.where(allowed[:, None, None, :], scores, -jnp.inf)
    new_max = jnp.maximum(run_max, jnp.max(scores, axis=-1))
    safe_max = jnp.where(new_max == -jnp.inf, 0.0, new_max)
    prob_vals = jnp.exp(scores - safe_max[..., None])
    rescale = jnp.exp(run_max - safe_max)
    run_sum = run_sum * rescale + jnp.sum(prob_vals, axis=-1)
    out_acc = out_acc * rescale[..., None] + jnp.einsum('qhgk,khd->qhgd', prob_vals.astype(jnp.bfloat16), v_blk, preferred_element_type=jnp.float32)
    return new_max, run_sum, out_acc


def solution(mesh):
    cp_size = mesh.shape['cp']
    shift_pairs = [(dev_idx, (dev_idx + 1) % cp_size) for dev_idx in range(cp_size)]

    def local_attention(x_loc, seg_loc, w_query, w_key, w_value, w_out):
        chunk_len = x_loc.shape[0]
        kv_heads = w_key.shape[1] // HEAD_DIM
        q_per_kv = w_query.shape[1] // w_key.shape[1]
        cp_rank = lax.axis_index('cp')
        q_loc = jnp.dot(x_loc, w_query, preferred_element_type=jnp.float32).astype(jnp.bfloat16).reshape(chunk_len, kv_heads, q_per_kv, HEAD_DIM)
        k_loc = jnp.dot(x_loc, w_key, preferred_element_type=jnp.float32).astype(jnp.bfloat16).reshape(chunk_len, kv_heads, HEAD_DIM)
        v_loc = jnp.dot(x_loc, w_value, preferred_element_type=jnp.float32).astype(jnp.bfloat16).reshape(chunk_len, kv_heads, HEAD_DIM)
        q_pos = cp_rank * chunk_len + jnp.arange(chunk_len)

        def visit_block(soft_state, k_blk, v_blk, seg_kv, src_chunk):
            k_pos = src_chunk * chunk_len + jnp.arange(chunk_len)
            active = (src_chunk <= cp_rank) & (seg_kv[chunk_len - 1] >= seg_loc[0])
            allowed = (seg_loc[:, None] == seg_kv[None, :]) & (q_pos[:, None] >= k_pos[None, :])
            return lax.cond(active, lambda same_state: block_update(same_state, q_loc, k_blk, v_blk, allowed), lambda same_state: same_state, soft_state)

        init_state = (jnp.full((chunk_len, kv_heads, q_per_kv), -jnp.inf, jnp.float32), jnp.zeros((chunk_len, kv_heads, q_per_kv), jnp.float32), jnp.zeros((chunk_len, kv_heads, q_per_kv, HEAD_DIM), jnp.float32))
        soft_state = visit_block(init_state, k_loc, v_loc, seg_loc, cp_rank)

        def shift_step(step_idx, loop_state):
            soft_state, k_blk, v_blk, seg_kv = loop_state
            k_blk = lax.ppermute(k_blk, 'cp', shift_pairs)
            v_blk = lax.ppermute(v_blk, 'cp', shift_pairs)
            seg_kv = lax.ppermute(seg_kv, 'cp', shift_pairs)
            src_chunk = (cp_rank - step_idx) % cp_size
            soft_state = visit_block(soft_state, k_blk, v_blk, seg_kv, src_chunk)
            return soft_state, k_blk, v_blk, seg_kv

        soft_state = lax.fori_loop(1, cp_size, shift_step, (soft_state, k_loc, v_loc, seg_loc))[0]
        heads_out = (soft_state[2] / soft_state[1][..., None]).astype(jnp.bfloat16).reshape(chunk_len, kv_heads * q_per_kv * HEAD_DIM)
        part_out = jnp.dot(heads_out, w_out, preferred_element_type=jnp.float32)
        return lax.psum(part_out, 'tp').astype(jnp.bfloat16)

    return jax.shard_map(local_attention, mesh=mesh, in_specs=(P(('dp', 'cp'), None), P(('dp', 'cp')), P(None, 'tp'), P(None, 'tp'), P(None, 'tp'), P('tp', None)), out_specs=P(('dp', 'cp'), None), check_vma=False)
```

profile of v0, /device:TPU:2, one launch (start us, length us, event | category | flops | bytes accessed | tf_op | source)
XLA Modules:
  0.0 551.1 jit_solution(4988938158762185396)
XLA Ops:
  0.0 1.3 fusion.48
  3.2 10.3 %convolution_convert_fusion.2 = bf16[512,512]{0,1:T(8,128)(2,1)S(1)} fusion(bf16[512,8192]{1,0:T(8,128)(2,1)} %param.12, bf16[8192,512]{1,0:T(8,128)(2,1)} %param.14), kind=kOutput, calls=%fused_computation.56 | convolution fusion | flops 4295229440 | bytes 17301504 | tf_op jit(solution)/shard_map/dot_general | solution.py:31
  13.8 10.3 %convolution_convert_fusion.1 = bf16[512,512]{0,1:T(8,128)(2,1)S(1)} fusion(bf16[512,8192]{1,0:T(8,128)(2,1)} %param.12, bf16[8192,512]{1,0:T(8,128)(2,1)} %param.15), kind=kOutput, calls=%fused_computation.55 | convolution fusion | flops 4295229440 | bytes 17301504 | tf_op jit(solution)/shard_map/dot_general | solution.py:32
  24.4 10.5 %convolution_convert_fusion = bf16[512,512]{0,1:T(8,128)(2,1)S(1)} fusion(bf16[512,8192]{1,0:T(8,128)(2,1)} %param.12, bf16[8192,512]{1,0:T(8,128)(2,1)} %param.16), kind=kOutput, calls=%fused_computation.54 | convolution fusion | flops 4295229440 | bytes 17301504 | tf_op jit(solution)/shard_map/dot_general | solution.py:33
  35.0 5.7 %conditional.2 = (f32[512,4,1]{0,1,2:T(4,128)}, f32[512,4,1]{0,1,2:T(4,128)S(1)}, f32[512,4,1,128]{3,0,1,2:T(8,128)S(1)}) conditional(s32[]{:T(128)} %bitcast.23, () %tuple.47, (s32[512]{0:T(512)S(1)}, s32[]{:T(128)}, s32[512,1]{0,1:T(1,128)S(1)}, s32[1,512]{1,0:T(1,128)S(1)}, bf16[512,4,1,128]{0,3,1,2:T(8,128)(2,1)S(1)}, ...), branch_computations={%region_0.0_spmd, %region_1.4_spmd} | conditional | flops 549469184 | bytes 16357408 | solution.py:40
  35.3 1.5 fusion.4
  37.5 0.9 fusion.3
  38.5 1.5 fusion.15
  40.7 1.0 copy.21
  41.7 135.4 %while.26 = (s32[]{:T(128)}, f32[512,4,1]{0,1,2:T(4,128)}, f32[512,4,1]{0,1,2:T(4,128)S(1)}, f32[512,4,1,128]{3,0,1,2:T(8,128)S(1)}, bf16[512,4,128]{2,0,1:T(8,1...) while((s32[]{:T(128)}, f32[512,4,1]{0,1,2:T(4,128)}, ...), condition=%wide.region_9.10_spmd.clone, body=%wide.region_4.9_spmd.clone.sunk | while | flops 549735424 | bytes 23773780 | solution.py:54
  41.7 1.6 collective-permute-start.1
  43.9 12.0 %collective-permute-done = s32[512]{0:T(512)S(1)} collective-permute-done((s32[512]{0:T(512)S(1)}, s32[512]{0:T(512)S(1)}, u32[]{:S(2)}, u32[]{:S(2)}) %collective-permute-start) | collective-permute-done | bytes 2080 | tf_op jit(solution)/shard_map/while/body/eval_jaxpr/ppermute | solution.py:49
  57.8 5.7 %conditional.5 = ((f32[512,4,1]{0,1,2:T(4,128)}, f32[512,4,1]{0,1,2:T(4,128)S(1)}, f32[512,4,1,128]{3,0,1,2:T(8,128)S(1)})) conditional(s32[]{:T(128)} %convert_element_type.68, (f32[512,4,1]{0,1,2:T(4,128)}, f32[512,4,1]{0,1,2:T(4,128)S(1)}, f32[512,4,1,128]{3,0,1,2:T(8,128)S(1)}) %tuple.74, (s32[512]{0:T(512)S(1)}, s32[512]{0:T(512)S(1)}, ...), branch_computations={%region_5.5_spmd, %region_6.8_spmd} | conditional | flops 549735424 | bytes 17465396 | solution.py:40
  58.1 0.8 fusion.28
  59.0 0.7 fusion.45
  59.7 0.9 fusion.27
  60.6 1.6 fusion.39
  62.2 0.7 bitcast_add_fusion
  63.5 0.8 copy.59
  64.4 1.6 collective-permute-start.1
  66.6 12.0 %collective-permute-done = s32[512]{0:T(512)S(1)} collective-permute-done((s32[512]{0:T(512)S(1)}, s32[512]{0:T(512)S(1)}, u32[]{:S(2)}, u32[]{:S(2)}) %collective-permute-start) | collective-permute-done | bytes 2080 | tf_op jit(solution)/shard_map/while/body/eval_jaxpr/ppermute | solution.py:49
  80.5 5.7 %conditional.5 = ((f32[512,4,1]{0,1,2:T(4,128)}, f32[512,4,1]{0,1,2:T(4,128)S(1)}, f32[512,4,1,128]{3,0,1,2:T(8,128)S(1)})) conditional(s32[]{:T(128)} %convert_element_type.68, (f32[512,4,1]{0,1,2:T(4,128)}, f32[512,4,1]{0,1,2:T(4,128)S(1)}, f32[512,4,1,128]{3,0,1,2:T(8,128)S(1)}) %tuple.74, (s32[512]{0:T(512)S(1)}, s32[512]{0:T(512)S(1)}, ...), branch_computations={%region_5.5_spmd, %region_6.8_spmd} | conditional | flops 549735424 | bytes 17465396 | solution.py:40
  80.9 0.8 fusion.28
  82.4 0.9 fusion.27
  83.3 1.6 fusion.39
  84.9 0.7 bitcast_add_fusion
  86.3 0.8 copy.59
  87.1 1.6 collective-permute-start.1
  89.3 12.0 %collective-permute-done = s32[512]{0:T(512)S(1)} collective-permute-done((s32[512]{0:T(512)S(1)}, s32[512]{0:T(512)S(1)}, u32[]{:S(2)}, u32[]{:S(2)}) %collective-permute-start) | collective-permute-done | bytes 2080 | tf_op jit(solution)/shard_map/while/body/eval_jaxpr/ppermute | solution.py:49
  103.3 0.8 copy.59
  104.1 4.8 collective-permute-start.2
  108.9 2.5 collective-permute-start.1
  112.1 6.3 %collective-permute-done = s32[512]{0:T(512)S(1)} collective-permute-done((s32[512]{0:T(512)S(1)}, s32[512]{0:T(512)S(1)}, u32[]{:S(2)}, u32[]{:S(2)}) %collective-permute-start) | collective-permute-done | bytes 2080 | tf_op jit(solution)/shard_map/while/body/eval_jaxpr/ppermute | solution.py:49
  120.3 0.8 copy.59
  121.1 4.8 collective-permute-start.2
  126.0 8.2 %collective-permute-start.1 = (bf16[512,4,128]{2,0,1:T(8,128)(2,1)S(1)}, bf16[512,4,128]{2,0,1:T(8,128)(2,1)S(1)}, u32[]{:S(2)}, u32[]{:S(2)}) collective-permute-start(bf16[512,4,128]{2,0,1:T(8,128)(2,1)S(1)} %get-tuple-element.609), channel_id=1, source_target_pairs={{0,1},{1,2},{2,3},{3,4},{4,5},{5,6},{6,7},{7,0},{8,9},{9,10},{10,1... | collective-permute-start | bytes 1572872 | tf_op jit(solution)/shard_map/while/body/eval_jaxpr/ppermute | solution.py:47
  134.8 2.4 collective-permute-done
  139.1 0.8 copy.59
  139.9 8.7 %collective-permute-start.2 = (bf16[512,4,128]{2,0,1:T(8,128)(2,1)}, bf16[512,4,128]{2,0,1:T(8,128)(2,1)S(1)}, u32[]{:S(2)}, u32[]{:S(2)}) collective-permute-start(bf16[512,4,128]{2,0,1:T(8,128)(2,1)} %get-tuple-element.610), channel_id=1, source_target_pairs={{0,1},{1,2},{2,3},{3,4},{4,5},{5,6},{6,7},{7,0},{8,9},{9,10},{10,1... | collective-permute-start | bytes 1572872 | tf_op jit(solution)/shard_map/while/body/eval_jaxpr/ppermute | solution.py:48
  148.7 2.5 collective-permute-start.1
  151.8 5.5 collective-permute-done
  159.2 0.8 copy.59
  160.1 5.6 %collective-permute-start.2 = (bf16[512,4,128]{2,0,1:T(8,128)(2,1)}, bf16[512,4,128]{2,0,1:T(8,128)(2,1)S(1)}, u32[]{:S(2)}, u32[]{:S(2)}) collective-permute-start(bf16[512,4,128]{2,0,1:T(8,128)(2,1)} %get-tuple-element.610), channel_id=1, source_target_pairs={{0,1},{1,2},{2,3},{3,4},{4,5},{5,6},{6,7},{7,0},{8,9},{9,10},{10,1... | collective-permute-start | bytes 1572872 | tf_op jit(solution)/shard_map/while/body/eval_jaxpr/ppermute | solution.py:48
  165.7 2.5 collective-permute-start.1
  168.8 5.5 collective-permute-done
  176.2 0.8 copy.59
  177.6 11.5 %fusion.49 = f32[512,8192]{1,0:T(8,128)} fusion(bf16[512,512]{0,1:T(8,128)(2,1)S(1)} %bitcast.112, bf16[512,8192]{1,0:T(8,128)(2,1)} %param.17), kind=kOutput, calls=%fused_computation.59 | convolution fusion | flops 4294967296 | bytes 25690112 | tf_op jit(solution)/shard_map/dot_general | solution.py:56
  189.1 362.1 %all-reduce.1 = bf16[512,8192]{1,0:T(8,128)(2,1)} all-reduce(f32[512,8192]{1,0:T(8,128)} %fusion.49), channel_id=1, replica_groups=mesh['dp'=1,'tp'=16,'cp'=8] {'tp'}, use_global_device_ids=true, to_apply=%region_10.11 | all-reduce | flops 4194304 | bytes 25165824 | tf_op jit(solution)/shard_map/psum | solution.py:57
  (96 shorter events, 14.7 us)
Async XLA Ops:
  24.4 10.5 %copy-start = (s32[512]{0:T(512)S(1)}, s32[512]{0:T(512)}, u32[]{:S(2)}) copy-start(s32[512]{0:T(512)} %param.13) | copy-start | bytes 6148
  41.7 16.1 %collective-permute-start.2 = (bf16[512,4,128]{2,0,1:T(8,128)(2,1)}, bf16[512,4,128]{2,0,1:T(8,128)(2,1)S(1)}, u32[]{:S(2)}, u32[]{:S(2)}) collective-permute-start(bf16[512,4,128]{2,0,1:T(8,128)(2,1)} %get-tuple-element.610), channel_id=1, source_target_pairs={{0,1},{1,2},{2,3},{3,4},{4,5},{5,6},{6,7},{7,0},{8,9},{9,10},{10,1... | collective-permute-start | bytes 1572872 | tf_op jit(solution)/shard_map/while/body/eval_jaxpr/ppermute | solution.py:48
  41.7 16.1 %collective-permute-start.1 = (bf16[512,4,128]{2,0,1:T(8,128)(2,1)S(1)}, bf16[512,4,128]{2,0,1:T(8,128)(2,1)S(1)}, u32[]{:S(2)}, u32[]{:S(2)}) collective-permute-start(bf16[512,4,128]{2,0,1:T(8,128)(2,1)S(1)} %get-tuple-element.609), channel_id=1, source_target_pairs={{0,1},{1,2},{2,3},{3,4},{4,5},{5,6},{6,7},{7,0},{8,9},{9,10},{10,1... | collective-permute-start | bytes 1572872 | tf_op jit(solution)/shard_map/while/body/eval_jaxpr/ppermute | solution.py:47
  43.3 12.6 %collective-permute-start = (s32[512]{0:T(512)S(1)}, s32[512]{0:T(512)S(1)}, u32[]{:S(2)}, u32[]{:S(2)}) collective-permute-start(s32[512]{0:T(512)S(1)} %get-tuple-element.611), channel_id=1, source_target_pairs={{0,1},{1,2},{2,3},{3,4},{4,5},{5,6},{6,7},{7,0},{8,9},{9,10},{10,1... | collective-permute-start | bytes 6152 | tf_op jit(solution)/shard_map/while/body/eval_jaxpr/ppermute | solution.py:49
  64.4 16.1 %collective-permute-start.2 = (bf16[512,4,128]{2,0,1:T(8,128)(2,1)}, bf16[512,4,128]{2,0,1:T(8,128)(2,1)S(1)}, u32[]{:S(2)}, u32[]{:S(2)}) collective-permute-start(bf16[512,4,128]{2,0,1:T(8,128)(2,1)} %get-tuple-element.610), channel_id=1, source_target_pairs={{0,1},{1,2},{2,3},{3,4},{4,5},{5,6},{6,7},{7,0},{8,9},{9,10},{10,1... | collective-permute-start | bytes 1572872 | tf_op jit(solution)/shard_map/while/body/eval_jaxpr/ppermute | solution.py:48
  64.4 16.1 %collective-permute-start.1 = (bf16[512,4,128]{2,0,1:T(8,128)(2,1)S(1)}, bf16[512,4,128]{2,0,1:T(8,128)(2,1)S(1)}, u32[]{:S(2)}, u32[]{:S(2)}) collective-permute-start(bf16[512,4,128]{2,0,1:T(8,128)(2,1)S(1)} %get-tuple-element.609), channel_id=1, source_target_pairs={{0,1},{1,2},{2,3},{3,4},{4,5},{5,6},{6,7},{7,0},{8,9},{9,10},{10,1... | collective-permute-start | bytes 1572872 | tf_op jit(solution)/shard_map/while/body/eval_jaxpr/ppermute | solution.py:47
  66.0 12.6 %collective-permute-start = (s32[512]{0:T(512)S(1)}, s32[512]{0:T(512)S(1)}, u32[]{:S(2)}, u32[]{:S(2)}) collective-permute-start(s32[512]{0:T(512)S(1)} %get-tuple-element.611), channel_id=1, source_target_pairs={{0,1},{1,2},{2,3},{3,4},{4,5},{5,6},{6,7},{7,0},{8,9},{9,10},{10,1... | collective-permute-start | bytes 6152 | tf_op jit(solution)/shard_map/while/body/eval_jaxpr/ppermute | solution.py:49
  87.1 16.1 %collective-permute-start.2 = (bf16[512,4,128]{2,0,1:T(8,128)(2,1)}, bf16[512,4,128]{2,0,1:T(8,128)(2,1)S(1)}, u32[]{:S(2)}, u32[]{:S(2)}) collective-permute-start(bf16[512,4,128]{2,0,1:T(8,128)(2,1)} %get-tuple-element.610), channel_id=1, source_target_pairs={{0,1},{1,2},{2,3},{3,4},{4,5},{5,6},{6,7},{7,0},{8,9},{9,10},{10,1... | collective-permute-start | bytes 1572872 | tf_op jit(solution)/shard_map/while/body/eval_jaxpr/ppermute | solution.py:48
  87.1 16.1 %collective-permute-start.1 = (bf16[512,4,128]{2,0,1:T(8,128)(2,1)S(1)}, bf16[512,4,128]{2,0,1:T(8,128)(2,1)S(1)}, u32[]{:S(2)}, u32[]{:S(2)}) collective-permute-start(bf16[512,4,128]{2,0,1:T(8,128)(2,1)S(1)} %get-tuple-element.609), channel_id=1, source_target_pairs={{0,1},{1,2},{2,3},{3,4},{4,5},{5,6},{6,7},{7,0},{8,9},{9,10},{10,1... | collective-permute-start | bytes 1572872 | tf_op jit(solution)/shard_map/while/body/eval_jaxpr/ppermute | solution.py:47
  88.7 12.6 %collective-permute-start = (s32[512]{0:T(512)S(1)}, s32[512]{0:T(512)S(1)}, u32[]{:S(2)}, u32[]{:S(2)}) collective-permute-start(s32[512]{0:T(512)S(1)} %get-tuple-element.611), channel_id=1, source_target_pairs={{0,1},{1,2},{2,3},{3,4},{4,5},{5,6},{6,7},{7,0},{8,9},{9,10},{10,1... | collective-permute-start | bytes 6152 | tf_op jit(solution)/shard_map/while/body/eval_jaxpr/ppermute | solution.py:49
  104.1 16.1 %collective-permute-start.2 = (bf16[512,4,128]{2,0,1:T(8,128)(2,1)}, bf16[512,4,128]{2,0,1:T(8,128)(2,1)S(1)}, u32[]{:S(2)}, u32[]{:S(2)}) collective-permute-start(bf16[512,4,128]{2,0,1:T(8,128)(2,1)} %get-tuple-element.610), channel_id=1, source_target_pairs={{0,1},{1,2},{2,3},{3,4},{4,5},{5,6},{6,7},{7,0},{8,9},{9,10},{10,1... | collective-permute-start | bytes 1572872 | tf_op jit(solution)/shard_map/while/body/eval_jaxpr/ppermute | solution.py:48
  108.9 11.3 %collective-permute-start.1 = (bf16[512,4,128]{2,0,1:T(8,128)(2,1)S(1)}, bf16[512,4,128]{2,0,1:T(8,128)(2,1)S(1)}, u32[]{:S(2)}, u32[]{:S(2)}) collective-permute-start(bf16[512,4,128]{2,0,1:T(8,128)(2,1)S(1)} %get-tuple-element.609), channel_id=1, source_target_pairs={{0,1},{1,2},{2,3},{3,4},{4,5},{5,6},{6,7},{7,0},{8,9},{9,10},{10,1... | collective-permute-start | bytes 1572872 | tf_op jit(solution)/shard_map/while/body/eval_jaxpr/ppermute | solution.py:47
  111.4 6.9 %collective-permute-start = (s32[512]{0:T(512)S(1)}, s32[512]{0:T(512)S(1)}, u32[]{:S(2)}, u32[]{:S(2)}) collective-permute-start(s32[512]{0:T(512)S(1)} %get-tuple-element.611), channel_id=1, source_target_pairs={{0,1},{1,2},{2,3},{3,4},{4,5},{5,6},{6,7},{7,0},{8,9},{9,10},{10,1... | collective-permute-start | bytes 6152 | tf_op jit(solution)/shard_map/while/body/eval_jaxpr/ppermute | solution.py:49
  121.1 17.9 %collective-permute-start.2 = (bf16[512,4,128]{2,0,1:T(8,128)(2,1)}, bf16[512,4,128]{2,0,1:T(8,128)(2,1)S(1)}, u32[]{:S(2)}, u32[]{:S(2)}) collective-permute-start(bf16[512,4,128]{2,0,1:T(8,128)(2,1)} %get-tuple-element.610), channel_id=1, source_target_pairs={{0,1},{1,2},{2,3},{3,4},{4,5},{5,6},{6,7},{7,0},{8,9},{9,10},{10,1... | collective-permute-start | bytes 1572872 | tf_op jit(solution)/shard_map/while/body/eval_jaxpr/ppermute | solution.py:48
  126.0 13.1 %collective-permute-start.1 = (bf16[512,4,128]{2,0,1:T(8,128)(2,1)S(1)}, bf16[512,4,128]{2,0,1:T(8,128)(2,1)S(1)}, u32[]{:S(2)}, u32[]{:S(2)}) collective-permute-start(bf16[512,4,128]{2,0,1:T(8,128)(2,1)S(1)} %get-tuple-element.609), channel_id=1, source_target_pairs={{0,1},{1,2},{2,3},{3,4},{4,5},{5,6},{6,7},{7,0},{8,9},{9,10},{10,1... | collective-permute-start | bytes 1572872 | tf_op jit(solution)/shard_map/while/body/eval_jaxpr/ppermute | solution.py:47
  134.2 3.0 collective-permute-start
  139.9 19.2 %collective-permute-start.2 = (bf16[512,4,128]{2,0,1:T(8,128)(2,1)}, bf16[512,4,128]{2,0,1:T(8,128)(2,1)S(1)}, u32[]{:S(2)}, u32[]{:S(2)}) collective-permute-start(bf16[512,4,128]{2,0,1:T(8,128)(2,1)} %get-tuple-element.610), channel_id=1, source_target_pairs={{0,1},{1,2},{2,3},{3,4},{4,5},{5,6},{6,7},{7,0},{8,9},{9,10},{10,1... | collective-permute-start | bytes 1572872 | tf_op jit(solution)/shard_map/while/body/eval_jaxpr/ppermute | solution.py:48
  148.7 10.5 %collective-permute-start.1 = (bf16[512,4,128]{2,0,1:T(8,128)(2,1)S(1)}, bf16[512,4,128]{2,0,1:T(8,128)(2,1)S(1)}, u32[]{:S(2)}, u32[]{:S(2)}) collective-permute-start(bf16[512,4,128]{2,0,1:T(8,128)(2,1)S(1)} %get-tuple-element.609), channel_id=1, source_target_pairs={{0,1},{1,2},{2,3},{3,4},{4,5},{5,6},{6,7},{7,0},{8,9},{9,10},{10,1... | collective-permute-start | bytes 1572872 | tf_op jit(solution)/shard_map/while/body/eval_jaxpr/ppermute | solution.py:47
  151.2 6.1 %collective-permute-start = (s32[512]{0:T(512)S(1)}, s32[512]{0:T(512)S(1)}, u32[]{:S(2)}, u32[]{:S(2)}) collective-permute-start(s32[512]{0:T(512)S(1)} %get-tuple-element.611), channel_id=1, source_target_pairs={{0,1},{1,2},{2,3},{3,4},{4,5},{5,6},{6,7},{7,0},{8,9},{9,10},{10,1... | collective-permute-start | bytes 6152 | tf_op jit(solution)/shard_map/while/body/eval_jaxpr/ppermute | solution.py:49
  160.1 16.1 %collective-permute-start.2 = (bf16[512,4,128]{2,0,1:T(8,128)(2,1)}, bf16[512,4,128]{2,0,1:T(8,128)(2,1)S(1)}, u32[]{:S(2)}, u32[]{:S(2)}) collective-permute-start(bf16[512,4,128]{2,0,1:T(8,128)(2,1)} %get-tuple-element.610), channel_id=1, source_target_pairs={{0,1},{1,2},{2,3},{3,4},{4,5},{5,6},{6,7},{7,0},{8,9},{9,10},{10,1... | collective-permute-start | bytes 1572872 | tf_op jit(solution)/shard_map/while/body/eval_jaxpr/ppermute | solution.py:48
  165.7 10.5 %collective-permute-start.1 = (bf16[512,4,128]{2,0,1:T(8,128)(2,1)S(1)}, bf16[512,4,128]{2,0,1:T(8,128)(2,1)S(1)}, u32[]{:S(2)}, u32[]{:S(2)}) collective-permute-start(bf16[512,4,128]{2,0,1:T(8,128)(2,1)S(1)} %get-tuple-element.609), channel_id=1, source_target_pairs={{0,1},{1,2},{2,3},{3,4},{4,5},{5,6},{6,7},{7,0},{8,9},{9,10},{10,1... | collective-permute-start | bytes 1572872 | tf_op jit(solution)/shard_map/while/body/eval_jaxpr/ppermute | solution.py:47
  168.2 6.1 %collective-permute-start = (s32[512]{0:T(512)S(1)}, s32[512]{0:T(512)S(1)}, u32[]{:S(2)}, u32[]{:S(2)}) collective-permute-start(s32[512]{0:T(512)S(1)} %get-tuple-element.611), channel_id=1, source_target_pairs={{0,1},{1,2},{2,3},{3,4},{4,5},{5,6},{6,7},{7,0},{8,9},{9,10},{10,1... | collective-permute-start | bytes 6152 | tf_op jit(solution)/shard_map/while/body/eval_jaxpr/ppermute | solution.py:49
where the time goes:
time: 557 us; the launch traced here: 551 us
  blocking collectives  362 us (65%)
  waiting for transfers between devices  55.8 us (10%)
  matrix products  50.5 us (9%)
  starting transfers between devices  44.7 us (8%)
  local copies, waits for them, and re-layouts  19.2 us (3%)
  loops' own time  9.56 us (2%)
  other arithmetic  8 us (1%)
    psum x1, blocking collectives, local_attention(): return lax.psum(part_out, 'tp').astype(jnp.bfloat16)  362 us
    ppermute x7, waiting for transfers between devices, shift_step(): seg_kv = lax.ppermute(seg_kv, 'cp', shift_pairs)  55.8 us
    ppermute x7, starting transfers between devices, shift_step(): v_blk = lax.ppermute(v_blk, 'cp', shift_pairs)  24 us
    ppermute x7, starting transfers between devices, shift_step(): k_blk = lax.ppermute(k_blk, 'cp', shift_pairs)  20.5 us
    dot_general x1, matrix products, local_attention(): part_out = jnp.dot(heads_out, w_out, preferred_element_type=jnp.float32)  11.5 us
  transfers between devices with their start and end apart: 21, of which 7 were waited for; matrix products, arithmetic and copies ran while one was open for 1% of the time, Pallas kernels for 0%

commit v1 on v0

v1 whole, which is shorter than its diff:
```python
import jax
import jax.numpy as jnp
from jax import lax
from jax.experimental import pallas as pl
from jax.experimental.pallas import tpu as pltpu
from jax.sharding import PartitionSpec as P

MESH = pl.DeviceIdType.MESH
HD = 128
NX = 4
L = 512
D = 8192
F = 512
KC = 1024
NKC = D // KC
NB = 4
PRE = 3
R = 4
RL = L // R
QT = 256
SCALE = (HD ** -0.5) * 1.4426950408889634
BF = jnp.bfloat16
F32 = jnp.float32


def mod(a, n):
    return lax.rem(a + n, n)


def kernel(x_hbm, seg_hbm, wq_hbm, wk_hbm, wv_hbm, wo_hbm, y_hbm,
           xbuf, wbuf, acc, kloc, vloc, qloc, kg, vg, qg, obuf, og, wt, psend, pown, rsb, yg, segs, sq, m_s, l_s, o_s,
           x_sem, w_sem, wo_sem, ws_send, ws_recv, wf_send, wf_recv,
           kv_send, kv_recv, kf_send, kf_recv, q_send, q_recv, o_send, o_recv,
           sg_send, sg_recv, sg_loc, a_send, a_recv, r_send, r_recv, y_send, y_recv, out_sem):
    t = lax.axis_index("tp")
    c = lax.axis_index("cp")
    x, k = c // 2, lax.rem(c, 2)
    z, y = t // NX, lax.rem(t, NX)
    yh, yb = y // 2, lax.rem(y, 2)
    xodd = lax.rem(x, 2)
    partner = {"cp": x * 2 + 1 - k}

    def iy(yy):
        return lax.rem(yy + yy // 2, 2)

    def slice_of(zz, yy):
        return zz * 2 + iy(yy)

    def piece_of(zz, yy):
        return slice_of(zz, yy) * 2 + yy // 2

    def tpdev(zz, yy):
        return {"tp": zz * NX + yy}

    def rcopy(src, dst, ss, rs, dev):
        return pltpu.make_async_remote_copy(src_ref=src, dst_ref=dst, send_sem=ss, recv_sem=rs, device_id=dev, device_id_type=MESH)

    s_me = z * 2 + yb
    sl_me = slice_of(z, y)
    sends = []

    def x_copy(i):
        return pltpu.make_async_copy(x_hbm.at[:, pl.ds(pl.multiple_of(i * KC, KC), KC)], xbuf.at[i], x_sem.at[i])

    w_hbms = (wk_hbm, wv_hbm, wq_hbm)

    def w_copy(w, i):
        slot = lax.rem(i, NB)
        return pltpu.make_async_copy(w_hbms[w].at[pl.ds(pl.multiple_of(i * KC, KC), KC), :], wbuf.at[slot], w_sem.at[slot])

    for i in range(PRE):
        x_copy(jnp.int32(i)).start()
        w_copy(0, jnp.int32(i)).start()
    seg_own = pltpu.make_async_copy(seg_hbm, segs.at[c], sg_loc)
    seg_own.start()
    wo_own = pltpu.make_async_copy(wo_hbm.at[:, pl.ds(pl.multiple_of(sl_me * 1024, 1024), 1024)],
                                   wt.at[pl.ds(pl.multiple_of(s_me * F, F), F), :], wo_sem)

    bar = pltpu.get_barrier_semaphore()
    n_peers = 0
    for dc in range(1, 2 * NX):
        pl.semaphore_signal(bar, inc=1, device_id={"cp": mod(c + dc, 2 * NX)}, device_id_type=MESH)
        n_peers += 1
    for dz in range(NX):
        for e in range(2):
            if dz or e:
                pl.semaphore_signal(bar, inc=1, device_id=tpdev(mod(z + dz, NX), yh * 2 + lax.rem(yb + e, 2)), device_id_type=MESH)
                n_peers += 1
    pl.semaphore_signal(bar, inc=1, device_id=tpdev(z, 3 - y), device_id_type=MESH)
    n_peers += 1
    pl.semaphore_wait(bar, n_peers)

    def w_move(dz, e):
        z2, y2 = mod(z + dz, NX), yh * 2 + lax.rem(yb + e, 2)
        i = dz * 2 + e - 1
        return rcopy(wo_hbm.at[pl.ds(pl.multiple_of(k * 256, 256), 256), pl.ds(pl.multiple_of(slice_of(z2, y2) * 1024, 1024), 1024)],
                     wt.at[pl.ds(pl.multiple_of(s_me * F + k * 256, 256), 256), :],
                     ws_send.at[i], ws_recv.at[i], tpdev(z2, y2))

    def w_rows(dz, e, kk):
        s = mod(z - dz, NX) * 2 + lax.rem(yb + e, 2)
        return wt.at[pl.ds(pl.multiple_of(s * F + kk * 256, 256), 256), :]

    def w_fwd(dz, e, kk):
        i = dz * 2 + e - 1
        ref = w_rows(dz, e, kk)
        return rcopy(ref, ref, wf_send.at[i], wf_recv.at[i], partner)

    group = [(dz, e) for dz in range(NX) for e in range(2) if dz or e]
    seg_own.wait()
    for dc in range(1, 2 * NX):
        cp_ = rcopy(segs.at[c], segs.at[c], sg_send.at[dc - 1], sg_recv.at[dc - 1], {"cp": mod(c + dc, 2 * NX)})
        cp_.start()
        sends.append(cp_)
    for dz, e in group:
        cp_ = w_move(dz, e)
        cp_.start()
        sends.append(cp_)
    wo_own.start()

    def project(w, lo, hi):
        def step(i, _):
            nxt = i + PRE

            @pl.when(nxt < NKC)
            def _():
                w_copy(w, nxt).start()
                if w == 0:
                    x_copy(nxt).start()
            if w < 2:
                @pl.when(nxt >= NKC)
                def _():
                    w_copy(w + 1, nxt - NKC).start()
            w_copy(w, i).wait()
            if w == 0:
                x_copy(i).wait()
            slot = lax.rem(i, NB)
            acc[...] += jnp.dot(xbuf[i], wbuf[slot], preferred_element_type=F32)
            return 0
        lax.fori_loop(lo, hi, step, 0)

    def split(dst):
        for h in range(4):
            dst[h] = acc[:, h * HD:(h + 1) * HD].astype(BF)

    def kv_spread(n, loc, gat):
        for dx in range(1, NX):
            h = mod(x + dx, NX)
            cp_ = rcopy(loc.at[h], gat.at[c], kv_send.at[n, dx - 1], kv_recv.at[n, dx - 1], {"cp": h * 2 + k})
            cp_.start()
            sends.append(cp_)
        cp_ = rcopy(loc.at[x], gat.at[c], kv_send.at[n, 3], kv_recv.at[n, 3], partner)
        cp_.start()
        sends.append(cp_)
        gat[c] = loc[x]

    def kv_forward(n, gat):
        for dx in (1, 3, 2):
            ref = gat.at[mod(x - dx, NX) * 2 + k]
            rcopy(ref, ref, kv_send.at[n, dx - 1], kv_recv.at[n, dx - 1], partner).wait_recv()
            cp_ = rcopy(ref, ref, kf_send.at[n, dx - 1], kf_recv.at[n, dx - 1], partner)
            cp_.start()
            sends.append(cp_)

    def kv_finish(n, gat):
        ref = gat.at[x * 2 + 1 - k]
        rcopy(ref, ref, kv_send.at[n, 3], kv_recv.at[n, 3], partner).wait_recv()
        for dx in (1, 3, 2):
            ref = gat.at[mod(x - dx, NX) * 2 + 1 - k]
            rcopy(ref, ref, kf_send.at[n, dx - 1], kf_recv.at[n, dx - 1], partner).wait_recv()

    acc[...] = jnp.zeros_like(acc)
    project(0, 0, NKC)
    split(kloc)
    acc[...] = jnp.zeros_like(acc)
    kv_spread(0, kloc, kg)
    project(1, 0, NKC)
    split(vloc)
    acc[...] = jnp.zeros_like(acc)
    kv_spread(1, vloc, vg)
    project(2, 0, NKC // 2)
    kv_forward(0, kg)
    project(2, NKC // 2, NKC)
    split(qloc)
    own = lax.rem(x + k, 2)
    for dx in (2, 1, 3):
        h = mod(x + dx, NX)
        cp_ = rcopy(qloc.at[h], qg.at[x], q_send.at[dx - 1], q_recv.at[x], {"cp": h * 2 + own})
        cp_.start()
        sends.append(cp_)

    @pl.when(xodd == 0)
    def _():
        qg[x] = qloc[x]

    q_d2d = rcopy(qloc.at[x], qg.at[x], q_send.at[3], q_recv.at[x], partner)

    @pl.when(xodd == 1)
    def _():
        q_d2d.start()

    kv_forward(1, vg)

    kv_finish(0, kg)
    kv_finish(1, vg)
    for dc in range(1, 2 * NX):
        ref = segs.at[mod(c - dc, 2 * NX)]
        rcopy(ref, ref, sg_send.at[dc - 1], sg_recv.at[dc - 1], partner).wait_recv()

    for xx in range(NX):
        c_q = 2 * xx + lax.rem(k + xx, 2)
        local = (x == xx) & (xodd == 0)

        @pl.when(jnp.logical_not(local))
        def _():
            rcopy(qg.at[xx], qg.at[xx], q_send.at[3], q_recv.at[xx], partner).wait_recv()

        sq[...] = jnp.transpose(jnp.broadcast_to(segs[c_q][0:1, :], (HD, L)))

        for qt in range(L // QT):
            rows = slice(qt * QT, (qt + 1) * QT)
            q_t = qg[xx, rows, :]
            sq_t = jnp.concatenate([sq[rows, :]] * (L // HD), axis=1)

            def scores(j):
                s = lax.dot_general(q_t, kg[j], (((1,), (1,)), ((), ())), preferred_element_type=F32) * SCALE
                return s, sq_t == jnp.broadcast_to(segs[j][0:1, :], (QT, L))

            s, ok = scores(c_q)
            ri = lax.broadcasted_iota(jnp.int32, (QT, L), 0) + qt * QT
            ci = lax.broadcasted_iota(jnp.int32, (QT, L), 1)
            s = jnp.where(ok & (ri >= ci), s, -jnp.inf)
            m0 = jnp.broadcast_to(jnp.max(s, axis=1, keepdims=True), (QT, HD))
            p = jnp.exp2(s - jnp.concatenate([m0] * (L // HD), axis=1))
            m_s[rows, :] = m0
            l_s[rows, :] = jnp.broadcast_to(jnp.sum(p, axis=1, keepdims=True), (QT, HD))
            o_s[rows, :] = jnp.dot(p.astype(BF), vg[c_q], preferred_element_type=F32)

            def kv_step(j, _):
                s, ok = scores(j)
                s = jnp.where(ok, s, -jnp.inf)
                m_old = m_s[rows, :]
                m_new = jnp.maximum(m_old, jnp.max(s, axis=1, keepdims=True))
                alpha = jnp.exp2(m_old - m_new)
                p = jnp.exp2(s - jnp.concatenate([m_new] * (L // HD), axis=1))
                m_s[rows, :] = m_new
                l_s[rows, :] = l_s[rows, :] * alpha + jnp.sum(p, axis=1, keepdims=True)
                o_s[rows, :] = o_s[rows, :] * alpha + jnp.dot(p.astype(BF), vg[j], preferred_element_type=F32)
                return 0
            lax.fori_loop(0, c_q, kv_step, 0)
            obuf[xx, rows, :] = (o_s[rows, :] / l_s[rows, :]).astype(BF)

        ocol = pl.ds(pl.multiple_of(s_me * F + x * HD, HD), HD)
        o_ret = rcopy(obuf.at[xx], og.at[:, ocol], o_send.at[xx], o_recv.at[x], {"cp": c_q})

        @pl.when(local)
        def _():
            og[:, ocol] = obuf[xx]

        @pl.when(jnp.logical_not(local))
        def _():
            o_ret.start()

    for h in range(NX):
        ref = og.at[:, pl.ds(pl.multiple_of(s_me * F + h * HD, HD), HD)]

        @pl.when(jnp.logical_not((x == h) & (xodd == 0)))
        def _():
            rcopy(obuf.at[0], ref, o_send.at[0], o_recv.at[h], partner).wait_recv()

    def o_ref(r, zz, e):
        s = zz * 2 + lax.rem(yb + e, 2)
        return og.at[pl.ds(r * RL, RL), pl.ds(pl.multiple_of(s * F, F), F)]

    def o_copy(r, idx, zz, e, dev):
        ref = o_ref(r, zz, e)
        return rcopy(ref, ref, a_send.at[r, idx], a_recv.at[r, idx], dev)

    def go(cp_):
        cp_.start()
        sends.append(cp_)

    def od(r):
        return 1 if r % 2 == 0 else NX - 1

    def o_send_z(r, e):
        d = od(r)
        go(o_copy(r, 1 + 3 * e, z, e, tpdev(mod(z + d, NX), y)))
        go(o_copy(r, 2 + 3 * e, z, e, tpdev(mod(z + NX - d, NX), y)))

    def o_mid_z(r, e):
        d = od(r)
        zz = mod(z + NX - d, NX)
        o_copy(r, 1 + 3 * e, zz, e, partner).wait_recv()
        go(o_copy(r, 3 + 3 * e, zz, e, tpdev(mod(z + d, NX), y)))

    def o_end_z(r, e):
        d = od(r)
        o_copy(r, 2 + 3 * e, mod(z + d, NX), e, partner).wait_recv()
        o_copy(r, 3 + 3 * e, mod(z + 2, NX), e, partner).wait_recv()

    pair = tpdev(z, yh * 2 + 1 - yb)
    for r in range(R):
        go(o_copy(r, 0, z, 0, pair))
        o_send_z(r, 0)

    for dz, e in group:
        ref = w_rows(dz, e, k)
        i = dz * 2 + e - 1
        rcopy(ref, ref, ws_send.at[i], ws_recv.at[i], partner).wait_recv()
        go(w_fwd(dz, e, k))

    def y_ref(r, zz, yy):
        return yg.at[pl.ds(r * RL, RL), pl.ds(pl.multiple_of(piece_of(zz, yy) * F, F), F)]

    def y_pos(r, a, b):
        if r % 2 == 0:
            return mod(z + a, NX), mod(y + b, NX)
        return mod(z + b, NX), mod(y + a, NX)

    def y_dir(r):
        return (1, NX - 1) if r < 2 else (NX - 1, 1)

    def y_copy(r, idx, pos, dev):
        ref = y_ref(r, *pos)
        return rcopy(ref, ref, y_send.at[r, idx], y_recv.at[r, idx], dev)

    def y_second(r, j, a):
        d2 = y_dir(r)[1]
        pos = y_pos(r, a, 0)
        go(y_copy(r, 3 + 3 * j, pos, tpdev(*y_pos(r, 0, d2))))
        go(y_copy(r, 4 + 3 * j, pos, tpdev(*y_pos(r, 0, NX - d2))))

    def y_start(r):
        d = y_dir(r)[0]
        pos = y_pos(r, 0, 0)
        go(y_copy(r, 0, pos, tpdev(*y_pos(r, d, 0))))
        go(y_copy(r, 1, pos, tpdev(*y_pos(r, NX - d, 0))))
        y_second(r, 0, 0)

    def y_mid(r):
        d = y_dir(r)[0]
        y_copy(r, 0, y_pos(r, NX - d, 0), partner).wait_recv()
        go(y_copy(r, 2, y_pos(r, NX - d, 0), tpdev(*y_pos(r, d, 0))))
        y_second(r, 1, NX - d)
        y_copy(r, 1, y_pos(r, d, 0), partner).wait_recv()
        y_second(r, 2, d)
        y_copy(r, 2, y_pos(r, 2, 0), partner).wait_recv()
        y_second(r, 3, 2)

    def y_offs(r):
        d = y_dir(r)[0]
        return (0, NX - d, d, 2)

    def y_fwd(r):
        d2 = y_dir(r)[1]
        for j, a in enumerate(y_offs(r)):
            pos = y_pos(r, a, NX - d2)
            y_copy(r, 3 + 3 * j, pos, partner).wait_recv()
            go(y_copy(r, 5 + 3 * j, pos, tpdev(*y_pos(r, 0, d2))))

    def y_end(r):
        d2 = y_dir(r)[1]
        for j, a in enumerate(y_offs(r)):
            y_copy(r, 4 + 3 * j, y_pos(r, a, d2), partner).wait_recv()
            y_copy(r, 5 + 3 * j, y_pos(r, a, 2), partner).wait_recv()
        out = pltpu.make_async_copy(yg.at[pl.ds(r * RL, RL), :], y_hbm.at[pl.ds(r * RL, RL), :], out_sem.at[r])
        out.start()
        return out

    def matmul(r, half):
        out = psend if half == 0 else pown
        hh = (1 - yh) if half == 0 else yh
        for n in range(2):
            cols = pl.ds(pl.multiple_of(hh * F + n * 256, 256), 256)
            out[r, :, n * 256:(n + 1) * 256] = jnp.dot(og[r * RL:(r + 1) * RL, :], wt[:, cols], preferred_element_type=F32)

    rs_dev = tpdev(z, 3 - y)

    def rs_copy(r):
        return rcopy(psend.at[r], rsb.at[r], r_send.at[r], r_recv.at[r], rs_dev)

    def rs_finish(r):
        rs_copy(r).wait_recv()
        yg[r * RL:(r + 1) * RL, pl.ds(pl.multiple_of(piece_of(z, y) * F, F), F)] = (pown[r] + rsb[r]).astype(BF)

    for r in range(R):
        o_copy(r, 0, z, 1, partner).wait_recv()
        o_send_z(r, 1)
        o_mid_z(r, 0)
    wo_own.wait()
    for dz, e in group:
        w_fwd(dz, e, 1 - k).wait_recv()
    for r in range(R):
        o_mid_z(r, 1)
        o_end_z(r, 0)
        o_end_z(r, 1)
        matmul(r, 0)
        go(rs_copy(r))
        matmul(r, 1)
        if r >= 1:
            rs_finish(r - 1)
            y_start(r - 1)
        if r >= 2:
            y_mid(r - 2)
    rs_finish(R - 1)
    y_start(R - 1)
    y_mid(R - 2)
    y_mid(R - 1)
    for r in range(R):
        y_fwd(r)
    outs = [y_end(r) for r in range(R)]

    for cp_ in sends:
        cp_.wait_send()

    @pl.when(xodd == 1)
    def _():
        q_d2d.wait_send()

    for xx in range(NX):
        @pl.when(jnp.logical_not((x == xx) & (xodd == 0)))
        def _():
            rcopy(obuf.at[xx], obuf.at[xx], o_send.at[xx], o_recv.at[x], partner).wait_send()
    for out in outs:
        out.wait()


def solution(mesh):
    def body(x, doc, wq, wk, wv, wo):
        seg = jnp.broadcast_to(doc[None, :], (8, L))
        dma = pltpu.SemaphoreType.DMA
        any_ = pl.BlockSpec(memory_space=pl.ANY)
        return pl.pallas_call(
            kernel,
            out_shape=jax.ShapeDtypeStruct((L, D), BF),
            in_specs=[any_] * 6,
            out_specs=any_,
            scratch_shapes=[
                pltpu.VMEM((NKC, L, KC), BF), pltpu.VMEM((NB, KC, F), BF), pltpu.VMEM((L, F), F32),
                pltpu.VMEM((4, L, HD), BF), pltpu.VMEM((4, L, HD), BF), pltpu.VMEM((4, L, HD), BF),
                pltpu.VMEM((8, L, HD), BF), pltpu.VMEM((8, L, HD), BF), pltpu.VMEM((4, L, HD), BF), pltpu.VMEM((4, L, HD), BF),
                pltpu.VMEM((L, 8 * F), BF), pltpu.VMEM((8 * F, 1024), BF),
                pltpu.VMEM((R, RL, F), F32), pltpu.VMEM((R, RL, F), F32), pltpu.VMEM((R, RL, F), F32),
                pltpu.VMEM((L, D), BF), pltpu.VMEM((8, 8, L), jnp.int32), pltpu.VMEM((L, HD), jnp.int32),
                pltpu.VMEM((L, HD), F32), pltpu.VMEM((L, HD), F32), pltpu.VMEM((L, HD), F32),
                dma((NKC,)), dma((NB,)), dma, dma((7,)), dma((7,)), dma((7,)), dma((7,)),
                dma((2, 4)), dma((2, 4)), dma((2, 3)), dma((2, 3)), dma((4,)), dma((4,)), dma((4,)), dma((4,)),
                dma((7,)), dma((7,)), dma, dma((R, 7)), dma((R, 7)), dma((R,)), dma((R,)), dma((R, 15)), dma((R, 15)), dma((R,)),
            ],
            compiler_params=pltpu.CompilerParams(collective_id=0, has_side_effects=True, vmem_limit_bytes=60 * 1024 * 1024),
        )(x, seg, wq, wk, wv, wo)

    return jax.shard_map(body, mesh=mesh, in_specs=(P(('dp', 'cp'), None), P(('dp', 'cp')), P(None, 'tp'), P(None, 'tp'), P(None, 'tp'), P('tp', None)), out_specs=P(('dp', 'cp'), None), check_vma=False)
```

time: 557 us -> 176 us (0.32)
  the two profiles are of different devices: /device:TPU:2 before, /device:TPU:30 now
where the time goes in v1:
time: 176 us
  Pallas kernels  167 us (95%)
  local copies, waits for them, and re-layouts  9.06 us (5%)
    pallas_call x1, Pallas kernels, body(): pl.pallas_call(kernel, out_shape=jax.ShapeDtypeStruct((L, D), BF), in_spe...  167 us
    unnamed x1, local copies, waits for them, and re-layouts  7.77 us

profile of v1, /device:TPU:30, one launch (start us, length us, event | category | flops | bytes accessed | tf_op | source)
XLA Modules:
  0.0 175.8 jit_solution(16996775647526348667)
XLA Ops:
  0.0 1.3 broadcast_in_dim.2.seg_hbm
  1.3 166.7 %shard_map.64 = bf16[512,8192]{1,0:T(8,128)(2,1)} custom-call(bf16[512,8192]{1,0:T(8,128)(2,1)} %x_hbm.1, s32[8,512]{1,0:T(8,128)} %broadcast_in_dim.2.seg_hbm, bf16[8192,512]{1,0:T(8,128)(2,1)} %wq_hbm.1, bf16[8192,512]{1,0:T(8,128)(2,1)} %wk_hbm.1, bf16[8192,512]{1,0:T(8,128)(2,1)} %wv_hbm.1, bf16[512,8192]{1,0:T(8,128)(2,1)} %wo_hbm.1), custom_call_target="tpu_custom_call" | custom-call | tf_op jit(solution)/shard_map/pallas_call | solution.py:434
  168.0 7.8 %copy.8 = bf16[512,8192]{1,0:T(8,128)(2,1)} copy(bf16[512,8192]{1,0:T(8,128)(2,1)} %shard_map.64) | data formatting | bytes 16777216

commit v2 on v1

v2 whole, which is shorter than its diff:
```python
import jax
import jax.numpy as jnp
from jax import lax
from jax.experimental import pallas as pl
from jax.experimental.pallas import tpu as pltpu
from jax.sharding import PartitionSpec as P

MESH = pl.DeviceIdType.MESH
HD = 128
NX = 4
L = 512
D = 8192
F = 512
KC = 1024
NKC = D // KC
NB = 6
ROWS = ((0, 64), (64, 64), (128, 128), (256, 128), (384, 64), (448, 64))
R = len(ROWS)
Y_ORDER = (0, 0, 1, 0, 1, 1)
Y_DIR = ((1, 3), (1, 3), (3, 1), (1, 1), (1, 3), (1, 3))
O_DIR = (1, 1, 3, 3, 1, 3)
ORDER = (
    ("ostart", 1), ("ostart", 5), ("ostart", 0), ("opair", 1), ("opair", 5), ("opair", 0),
    ("ofw0", 5), ("ofw1", 1), ("ofw1", 5), ("ofw0", 1), ("ofw0", 0), ("ostart", 2),
    ("ofw1", 0), ("mm0", 1), ("mm0", 5), ("opair", 2), ("ofw0", 2), ("mm1", 1),
    ("mm0", 0), ("ofw1", 2), ("ostart", 4), ("mm1", 0), ("mm1", 5), ("yst", 1),
    ("yst", 5), ("yst", 0), ("ofw0", 4), ("opair", 4), ("mm0", 2), ("mm1", 2),
    ("ostart", 3), ("ofw1", 4), ("opair", 3), ("ym0", 0), ("ym0", 1), ("ym1", 1),
    ("ofw0", 3), ("mm0", 4), ("mm1", 4), ("ofw1", 3), ("yst", 2), ("ym2", 1),
    ("ym1", 5), ("yst", 4), ("mm0", 3), ("ym0", 2), ("ym1", 0), ("ym0", 4),
    ("mm1", 3), ("ym2", 0), ("yf", 2, 0), ("yf", 1, 0), ("ym1", 4), ("yst", 3),
    ("ym0", 5), ("ym2", 4), ("yf", 0, 3), ("yf", 0, 2), ("yf", 5, 0), ("ym0", 3),
    ("yf", 0, 0), ("yf", 4, 3), ("ym2", 5), ("yf", 5, 1), ("ym2", 2), ("yf", 1, 2),
    ("yf", 4, 1), ("yf", 1, 3), ("yf", 4, 2), ("ym1", 3), ("ym1", 2), ("yf", 0, 1),
    ("yf", 3, 1), ("yf", 3, 0), ("yf", 1, 1), ("ym2", 3), ("yf", 2, 3), ("yf", 3, 2),
    ("yf", 2, 1), ("yf", 4, 0), ("yf", 5, 2), ("yf", 2, 2), ("yf", 5, 3), ("yf", 3, 3),
    ("ye", 2), ("ye", 0), ("ye", 5), ("ye", 4), ("ye", 1), ("ye", 3),
)
QT = 256
SCALE = (HD ** -0.5) * 1.4426950408889634
BF = jnp.bfloat16
F32 = jnp.float32


def mod(a, n):
    return lax.rem(a + n, n)


def kernel(x_hbm, seg_hbm, wq_hbm, wk_hbm, wv_hbm, wo_hbm, yg,
           xbuf, wbuf, acc, kloc, vloc, qloc, kg, vg, qg, obuf, og, wt, psend, pown, rsb, segs, sq, m_s, l_s, o_s,
           x_sem, w_sem, wo_sem, ws_send, ws_recv, wf_send, wf_recv,
           kv_send, kv_recv, kf_send, kf_recv, q_send, q_recv, o_send, o_recv,
           sg_send, sg_recv, sg_loc, a_send, a_recv, r_send, r_recv, y_send, y_recv):
    t = lax.axis_index("tp")
    c = lax.axis_index("cp")
    x, k = c // 2, lax.rem(c, 2)
    z, y = t // NX, lax.rem(t, NX)
    yh, yb = y // 2, lax.rem(y, 2)
    xodd = lax.rem(x, 2)
    partner = {"cp": x * 2 + 1 - k}

    def iy(yy):
        return lax.rem(yy + yy // 2, 2)

    def slice_of(zz, yy):
        return zz * 2 + iy(yy)

    def piece_of(zz, yy):
        return slice_of(zz, yy) * 2 + yy // 2

    def tpdev(zz, yy):
        return {"tp": zz * NX + yy}

    def rcopy(src, dst, ss, rs, dev):
        return pltpu.make_async_remote_copy(src_ref=src, dst_ref=dst, send_sem=ss, recv_sem=rs, device_id=dev, device_id_type=MESH)

    s_me = z * 2 + yb
    sl_me = slice_of(z, y)
    sends = []

    def x_copy(i):
        return pltpu.make_async_copy(x_hbm.at[:, pl.ds(pl.multiple_of(i * KC, KC), KC)], xbuf.at[i], x_sem.at[i])

    w_hbms = (wk_hbm, wv_hbm, wq_hbm)

    def w_copies(w, i):
        g = lax.rem(4 * w + i, 3) * 2
        return [pltpu.make_async_copy(w_hbms[w].at[pl.ds(pl.multiple_of((2 * i + b) * KC, KC), KC), :], wbuf.at[g + b], w_sem.at[g + b]) for b in range(2)]

    def load(w, i):
        for b, cp_ in enumerate(w_copies(w, i)):
            if w == 0:
                x_copy(2 * i + b).start()
            cp_.start()

    for i in range(2):
        load(0, jnp.int32(i))
    seg_own = pltpu.make_async_copy(seg_hbm, segs.at[c], sg_loc)
    seg_own.start()
    wo_own = pltpu.make_async_copy(wo_hbm.at[:, pl.ds(pl.multiple_of(sl_me * 1024, 1024), 1024)],
                                   wt.at[pl.ds(pl.multiple_of(s_me * F, F), F), :], wo_sem)

    bar = pltpu.get_barrier_semaphore()
    n_peers = 0
    for dc in range(1, 2 * NX):
        pl.semaphore_signal(bar, inc=1, device_id={"cp": mod(c + dc, 2 * NX)}, device_id_type=MESH)
        n_peers += 1
    for dz in range(NX):
        for e in range(2):
            if dz or e:
                pl.semaphore_signal(bar, inc=1, device_id=tpdev(mod(z + dz, NX), yh * 2 + lax.rem(yb + e, 2)), device_id_type=MESH)
                n_peers += 1
    pl.semaphore_signal(bar, inc=1, device_id=tpdev(z, 3 - y), device_id_type=MESH)
    n_peers += 1

    def w_move(dz, e):
        z2, y2 = mod(z + dz, NX), yh * 2 + lax.rem(yb + e, 2)
        i = dz * 2 + e - 1
        return rcopy(wo_hbm.at[pl.ds(pl.multiple_of(k * 256, 256), 256), pl.ds(pl.multiple_of(slice_of(z2, y2) * 1024, 1024), 1024)],
                     wt.at[pl.ds(pl.multiple_of(s_me * F + k * 256, 256), 256), :],
                     ws_send.at[i], ws_recv.at[i], tpdev(z2, y2))

    def w_rows(dz, e, kk):
        s = mod(z - dz, NX) * 2 + lax.rem(yb + e, 2)
        return wt.at[pl.ds(pl.multiple_of(s * F + kk * 256, 256), 256), :]

    def w_fwd(dz, e, kk):
        i = dz * 2 + e - 1
        ref = w_rows(dz, e, kk)
        return rcopy(ref, ref, wf_send.at[i], wf_recv.at[i], partner)

    group = [(dz, e) for dz in range(NX) for e in range(2) if dz or e]
    def spread_w():
        pl.semaphore_wait(bar, n_peers)
        seg_own.wait()
        for dc in range(1, 2 * NX):
            cp_ = rcopy(segs.at[c], segs.at[c], sg_send.at[dc - 1], sg_recv.at[dc - 1], {"cp": mod(c + dc, 2 * NX)})
            cp_.start()
            sends.append(cp_)
        for dz, e in group:
            cp_ = w_move(dz, e)
            cp_.start()
            sends.append(cp_)
        wo_own.start()

    def project(w, lo, hi):
        def step(i, _):
            nxt = i + 2

            @pl.when(nxt < NKC // 2)
            def _():
                load(w, nxt)
            if w < 2:
                @pl.when(nxt >= NKC // 2)
                def _():
                    load(w + 1, nxt - NKC // 2)
            for b, cp_ in enumerate(w_copies(w, i)):
                cp_.wait()
                if w == 0:
                    x_copy(2 * i + b).wait()
            g = lax.rem(4 * w + i, 3) * 2
            acc[...] += (jnp.dot(xbuf[2 * i], wbuf[g], preferred_element_type=F32)
                         + jnp.dot(xbuf[2 * i + 1], wbuf[g + 1], preferred_element_type=F32))
            return 0
        lax.fori_loop(lo, hi, step, 0)

    def split(dst):
        for h in range(4):
            dst[h] = acc[:, h * HD:(h + 1) * HD].astype(BF)

    def kv_spread(n, loc, gat):
        for dx in range(1, NX):
            h = mod(x + dx, NX)
            cp_ = rcopy(loc.at[h], gat.at[c], kv_send.at[n, dx - 1], kv_recv.at[n, dx - 1], {"cp": h * 2 + k})
            cp_.start()
            sends.append(cp_)
        cp_ = rcopy(loc.at[x], gat.at[c], kv_send.at[n, 3], kv_recv.at[n, 3], partner)
        cp_.start()
        sends.append(cp_)
        gat[c] = loc[x]

    def kv_forward(n, gat):
        for dx in (1, 3, 2):
            ref = gat.at[mod(x - dx, NX) * 2 + k]
            rcopy(ref, ref, kv_send.at[n, dx - 1], kv_recv.at[n, dx - 1], partner).wait_recv()
            cp_ = rcopy(ref, ref, kf_send.at[n, dx - 1], kf_recv.at[n, dx - 1], partner)
            cp_.start()
            sends.append(cp_)

    def kv_finish(n, gat):
        ref = gat.at[x * 2 + 1 - k]
        rcopy(ref, ref, kv_send.at[n, 3], kv_recv.at[n, 3], partner).wait_recv()
        for dx in (1, 3, 2):
            ref = gat.at[mod(x - dx, NX) * 2 + 1 - k]
            rcopy(ref, ref, kf_send.at[n, dx - 1], kf_recv.at[n, dx - 1], partner).wait_recv()

    acc[...] = jnp.zeros_like(acc)
    with jax.named_scope("proj_k0"):
        project(0, 0, 2)
    with jax.named_scope("barrier"):
        spread_w()
    with jax.named_scope("proj_k1"):
        project(0, 2, 4)
    split(kloc)
    acc[...] = jnp.zeros_like(acc)
    kv_spread(0, kloc, kg)
    with jax.named_scope("proj_v"):
        project(1, 0, 4)
    split(vloc)
    acc[...] = jnp.zeros_like(acc)
    kv_spread(1, vloc, vg)
    with jax.named_scope("proj_q0"):
        project(2, 0, 2)
    with jax.named_scope("fwd_k"):
        kv_forward(0, kg)
    with jax.named_scope("proj_q1"):
        project(2, 2, 4)
    split(qloc)
    own = lax.rem(x + k, 2)
    for dx in (2, 1, 3):
        h = mod(x + dx, NX)
        cp_ = rcopy(qloc.at[h], qg.at[x], q_send.at[dx - 1], q_recv.at[x], {"cp": h * 2 + own})
        cp_.start()
        sends.append(cp_)

    @pl.when(xodd == 0)
    def _():
        qg[x] = qloc[x]

    q_d2d = rcopy(qloc.at[x], qg.at[x], q_send.at[3], q_recv.at[x], partner)

    @pl.when(xodd == 1)
    def _():
        q_d2d.start()

    with jax.named_scope("fwd_v"):
        kv_forward(1, vg)

    with jax.named_scope("fin_kv"):
        kv_finish(0, kg)
        kv_finish(1, vg)
    for dc in range(1, 2 * NX):
        ref = segs.at[mod(c - dc, 2 * NX)]
        rcopy(ref, ref, sg_send.at[dc - 1], sg_recv.at[dc - 1], partner).wait_recv()

    for xx in range(NX):
        c_q = 2 * xx + lax.rem(k + xx, 2)
        local = (x == xx) & (xodd == 0)

        @pl.when(jnp.logical_not(local))
        def _():
            rcopy(qg.at[xx], qg.at[xx], q_send.at[3], q_recv.at[xx], partner).wait_recv()

        sq[...] = jnp.transpose(jnp.broadcast_to(segs[c_q], (HD, L)))

        def block(j, rows, diag):
            s = lax.dot_general(qg[xx, rows, :], kg[j], (((1,), (1,)), ((), ())), preferred_element_type=F32)
            ok = jnp.concatenate([sq[rows, :]] * (L // HD), axis=1) == jnp.broadcast_to(segs[j], (QT, L))
            if diag:
                ri = lax.broadcasted_iota(jnp.int32, (QT, L), 0) + rows.start
                ok = ok & (ri >= lax.broadcasted_iota(jnp.int32, (QT, L), 1))
            return jnp.where(ok, s * SCALE, -jnp.inf)

        tiles = [slice(a, a + QT) for a in range(0, L, QT)]
        with jax.named_scope("attn%d" % xx):
            for rows in tiles:
                s = block(c_q, rows, True)
                m0 = jnp.broadcast_to(jnp.max(s, axis=1, keepdims=True), (QT, HD))
                p = jnp.exp2(s - jnp.concatenate([m0] * (L // HD), axis=1))
                m_s[rows, :] = m0
                l_s[rows, :] = jnp.broadcast_to(jnp.sum(p, axis=1, keepdims=True), (QT, HD))
                o_s[rows, :] = jnp.dot(p.astype(BF), vg[c_q], preferred_element_type=F32)

            def kv_step(j, _):
                for rows in tiles:
                    s = block(j, rows, False)
                    m_old = m_s[rows, :]
                    m_new = jnp.maximum(m_old, jnp.max(s, axis=1, keepdims=True))
                    alpha = jnp.exp2(m_old - m_new)
                    p = jnp.exp2(s - jnp.concatenate([m_new] * (L // HD), axis=1))
                    m_s[rows, :] = m_new
                    l_s[rows, :] = l_s[rows, :] * alpha + jnp.sum(p, axis=1, keepdims=True)
                    o_s[rows, :] = o_s[rows, :] * alpha + jnp.dot(p.astype(BF), vg[j], preferred_element_type=F32)
                return 0
            lax.fori_loop(0, c_q, kv_step, 0)
            for rows in tiles:
                obuf[xx, rows, :] = (o_s[rows, :] / l_s[rows, :]).astype(BF)

        ocol = pl.ds(pl.multiple_of(s_me * F + x * HD, HD), HD)
        o_ret = rcopy(obuf.at[xx], og.at[:, ocol], o_send.at[xx], o_recv.at[x], {"cp": c_q})

        @pl.when(local)
        def _():
            og[:, ocol] = obuf[xx]

        @pl.when(jnp.logical_not(local))
        def _():
            o_ret.start()

    for h in range(NX):
        ref = og.at[:, pl.ds(pl.multiple_of(s_me * F + h * HD, HD), HD)]

        @pl.when(jnp.logical_not((x == h) & (xodd == 0)))
        def _():
            rcopy(obuf.at[0], ref, o_send.at[0], o_recv.at[h], partner).wait_recv()

    def go(cp_):
        cp_.start()
        sends.append(cp_)

    def row_ds(r):
        return pl.ds(ROWS[r][0], ROWS[r][1])

    def o_copy(r, idx, zz, e, dev):
        s = zz * 2 + lax.rem(yb + e, 2)
        ref = og.at[row_ds(r), pl.ds(pl.multiple_of(s * F, F), F)]
        return rcopy(ref, ref, a_send.at[r, idx], a_recv.at[r, idx], dev)

    def o_send_z(r, e):
        d = O_DIR[r]
        go(o_copy(r, 1 + 3 * e, z, e, tpdev(mod(z + d, NX), y)))
        go(o_copy(r, 2 + 3 * e, z, e, tpdev(mod(z + NX - d, NX), y)))

    def o_forward(r, e):
        d = O_DIR[r]
        zz = mod(z + NX - d, NX)
        o_copy(r, 1 + 3 * e, zz, e, partner).wait_recv()
        go(o_copy(r, 3 + 3 * e, zz, e, tpdev(mod(z + d, NX), y)))

    def ostart(r):
        go(o_copy(r, 0, z, 0, tpdev(z, yh * 2 + 1 - yb)))
        o_send_z(r, 0)

    def opair(r):
        o_copy(r, 0, z, 1, partner).wait_recv()
        o_send_z(r, 1)

    def o_rest(r):
        for e in range(2):
            o_copy(r, 2 + 3 * e, mod(z + O_DIR[r], NX), e, partner).wait_recv()
            o_copy(r, 3 + 3 * e, mod(z + 2, NX), e, partner).wait_recv()

    def matmul(r, half):
        out = psend if half == 0 else pown
        hh = (1 - yh) if half == 0 else yh
        a, n = ROWS[r]
        for b in range(2):
            cols = pl.ds(pl.multiple_of(hh * F + b * 256, 256), 256)
            out[a:a + n, b * 256:(b + 1) * 256] = jnp.dot(og[a:a + n, :], wt[:, cols], preferred_element_type=F32)

    def rs_copy(r):
        return rcopy(psend.at[row_ds(r), :], rsb.at[row_ds(r), :], r_send.at[r], r_recv.at[r], tpdev(z, 3 - y))

    def mm0(r):
        o_rest(r)
        if r == first_mm:
            wo_own.wait()
            for dz, e in group:
                w_fwd(dz, e, 1 - k).wait_recv()
        matmul(r, 0)
        go(rs_copy(r))

    def y_pos(r, a, b):
        if Y_ORDER[r] == 0:
            return mod(z + a, NX), mod(y + b, NX)
        return mod(z + b, NX), mod(y + a, NX)

    def y_ref(r, pos):
        return yg.at[row_ds(r), pl.ds(pl.multiple_of(piece_of(*pos) * F, F), F)]

    def y_copy(r, idx, pos, dev):
        ref = y_ref(r, pos)
        return rcopy(ref, ref, y_send.at[r, idx], y_recv.at[r, idx], dev)

    def y_second(r, j, a):
        d2 = Y_DIR[r][1]
        pos = y_pos(r, a, 0)
        go(y_copy(r, 3 + 3 * j, pos, tpdev(*y_pos(r, 0, d2))))
        go(y_copy(r, 4 + 3 * j, pos, tpdev(*y_pos(r, 0, NX - d2))))

    def yst(r):
        rs_copy(r).wait_recv()
        a, n = ROWS[r]
        yg[a:a + n, pl.ds(pl.multiple_of(piece_of(z, y) * F, F), F)] = (pown[a:a + n, :] + rsb[a:a + n, :]).astype(BF)
        d = Y_DIR[r][0]
        pos = y_pos(r, 0, 0)
        go(y_copy(r, 0, pos, tpdev(*y_pos(r, d, 0))))
        go(y_copy(r, 1, pos, tpdev(*y_pos(r, NX - d, 0))))
        y_second(r, 0, 0)

    def ym0(r):
        d = Y_DIR[r][0]
        pos = y_pos(r, NX - d, 0)
        y_copy(r, 0, pos, partner).wait_recv()
        go(y_copy(r, 2, pos, tpdev(*y_pos(r, d, 0))))
        y_second(r, 1, NX - d)

    def ym1(r):
        d = Y_DIR[r][0]
        y_copy(r, 1, y_pos(r, d, 0), partner).wait_recv()
        y_second(r, 2, d)

    def ym2(r):
        y_copy(r, 2, y_pos(r, 2, 0), partner).wait_recv()
        y_second(r, 3, 2)

    def y_offs(r):
        d = Y_DIR[r][0]
        return (0, NX - d, d, 2)

    def yf(r, j):
        d2 = Y_DIR[r][1]
        pos = y_pos(r, y_offs(r)[j], NX - d2)
        y_copy(r, 3 + 3 * j, pos, partner).wait_recv()
        go(y_copy(r, 5 + 3 * j, pos, tpdev(*y_pos(r, 0, d2))))

    def ye(r):
        d2 = Y_DIR[r][1]
        for j, a in enumerate(y_offs(r)):
            y_copy(r, 4 + 3 * j, y_pos(r, a, d2), partner).wait_recv()
            y_copy(r, 5 + 3 * j, y_pos(r, a, 2), partner).wait_recv()

    steps = dict(ostart=ostart, opair=opair, ofw0=lambda r: o_forward(r, 0), ofw1=lambda r: o_forward(r, 1), mm0=mm0,
                 mm1=lambda r: matmul(r, 1), yst=yst, ym0=ym0, ym1=ym1, ym2=ym2, yf=yf, ye=ye)
    first_mm = [a[1] for a in ORDER if a[0] == "mm0"][0]
    started = False
    for name, *args in ORDER:
        if not started and name != "ostart":
            started = True
            for dz, e in group:
                i = dz * 2 + e - 1
                with jax.named_scope("wait_w%d" % i):
                    ref = w_rows(dz, e, k)
                    rcopy(ref, ref, ws_send.at[i], ws_recv.at[i], partner).wait_recv()
                    go(w_fwd(dz, e, k))
        with jax.named_scope(name + "_".join(str(a) for a in args)):
            steps[name](*args)

    for cp_ in sends:
        cp_.wait_send()

    @pl.when(xodd == 1)
    def _():
        q_d2d.wait_send()

    for xx in range(NX):
        @pl.when(jnp.logical_not((x == xx) & (xodd == 0)))
        def _():
            rcopy(obuf.at[xx], obuf.at[xx], o_send.at[xx], o_recv.at[x], partner).wait_send()


def solution(mesh):
    def body(x, doc, wq, wk, wv, wo):
        seg = doc.reshape(1, L)
        dma = pltpu.SemaphoreType.DMA
        any_ = pl.BlockSpec(memory_space=pl.ANY)
        return pl.pallas_call(
            kernel,
            out_shape=pltpu.VMEM((L, D), BF),
            in_specs=[any_] * 6,
            out_specs=pl.BlockSpec(memory_space=pltpu.VMEM),
            scratch_shapes=[
                pltpu.VMEM((NKC, L, KC), BF), pltpu.VMEM((NB, KC, F), BF), pltpu.VMEM((L, F), F32),
                pltpu.VMEM((4, L, HD), BF), pltpu.VMEM((4, L, HD), BF), pltpu.VMEM((4, L, HD), BF),
                pltpu.VMEM((8, L, HD), BF), pltpu.VMEM((8, L, HD), BF), pltpu.VMEM((4, L, HD), BF), pltpu.VMEM((4, L, HD), BF),
                pltpu.VMEM((L, 8 * F), BF), pltpu.VMEM((8 * F, 1024), BF),
                pltpu.VMEM((L, F), F32), pltpu.VMEM((L, F), F32), pltpu.VMEM((L, F), F32),
                pltpu.VMEM((8, 1, L), jnp.int32), pltpu.VMEM((L, HD), jnp.int32),
                pltpu.VMEM((L, HD), F32), pltpu.VMEM((L, HD), F32), pltpu.VMEM((L, HD), F32),
                dma((NKC,)), dma((NB,)), dma, dma((7,)), dma((7,)), dma((7,)), dma((7,)),
                dma((2, 4)), dma((2, 4)), dma((2, 3)), dma((2, 3)), dma((4,)), dma((4,)), dma((4,)), dma((4,)),
                dma((7,)), dma((7,)), dma, dma((R, 7)), dma((R, 7)), dma((R,)), dma((R,)), dma((R, 15)), dma((R, 15)),
            ],
            compiler_params=pltpu.CompilerParams(collective_id=0, has_side_effects=True, vmem_limit_bytes=50 * 1024 * 1024),
        )(x, seg, wq, wk, wv, wo)

    return jax.shard_map(body, mesh=mesh, in_specs=(P(('dp', 'cp'), None), P(('dp', 'cp')), P(None, 'tp'), P(None, 'tp'), P(None, 'tp'), P('tp', None)), out_specs=P(('dp', 'cp'), None), check_vma=False)
```

time: 176 us -> 142 us (0.81)
  the two profiles are of different devices: /device:TPU:30 before, /device:TPU:2 now
where the time goes in v2:
time: 142 us
  Pallas kernels  139 us (98%)
  local copies, waits for them, and re-layouts  3.4 us (2%)
    pallas_call x1, Pallas kernels, body(): pl.pallas_call(kernel, out_shape=pltpu.VMEM((L, D), BF), in_specs=[any_]...  139 us
    unnamed x1, local copies, waits for them, and re-layouts  3.4 us

profile of v2, /device:TPU:2, one launch (start us, length us, event | category | flops | bytes accessed | tf_op | source)
XLA Modules:
  0.0 142.0 jit_solution(10948727401566005351)
XLA Ops:
  0.0 138.6 %shard_map.64 = bf16[512,8192]{1,0:T(8,128)(2,1)S(1)} custom-call(bf16[512,8192]{1,0:T(8,128)(2,1)} %x_hbm.1, s32[1,512]{1,0:T(1,128)} %bitcast.1, bf16[8192,512]{1,0:T(8,128)(2,1)} %wq_hbm.1, bf16[8192,512]{1,0:T(8,128)(2,1)} %wk_hbm.1, bf16[8192,512]{1,0:T(8,128)(2,1)} %wv_hbm.1, bf16[512,8192]{1,0:T(8,128)(2,1)} %wo_hbm.1), custom_call_target="tpu_custom_call" | custom-call | tf_op jit(solution)/shard_map/pallas_call | solution.py:457
  138.6 3.4 %copy.8 = bf16[512,8192]{1,0:T(8,128)(2,1)} copy(bf16[512,8192]{1,0:T(8,128)(2,1)S(1)} %shard_map.64) | data formatting | bytes 16777216

commit v3 on v2

v3 whole, which is shorter than its diff:
```python
import jax
import jax.numpy as jnp
from jax import lax
from jax.experimental import pallas as pl
from jax.experimental.pallas import tpu as pltpu
from jax.sharding import PartitionSpec as P

MESH = pl.DeviceIdType.MESH
HD = 128
NX = 4
L = 512
D = 8192
F = 512
KC = 1024
NKC = D // KC
NB = 6
ROWS = ((0, 64), (64, 64), (128, 64), (192, 64), (256, 64), (320, 64), (384, 64), (448, 64))
R = len(ROWS)
Y_ORDER = (1, 1, 0, 1, 1, 0, 1, 0)
Y_DIR = ((3, 1), (3, 1), (3, 1), (1, 3), (3, 3), (3, 3), (3, 1), (3, 1))
O_FIRST = (0, 1, 0, 1, 0, 1, 0, 0)
O_DIR = (1, 1, 3, 3, 3, 1, 3, 3)
ORDER = (
    ("ostart", 3,), ("ostart", 0,), ("ostart", 2,), ("opair", 3,), ("ostart", 1,), ("ofw0", 0,),
    ("ofw0", 3,), ("opair", 0,), ("opair", 2,), ("ofw1", 3,), ("opair", 1,), ("wxl",),
    ("ostart", 5,), ("ofw1", 0,), ("ostart", 7,), ("ofw0", 2,), ("ofw0", 1,), ("mm0", 3,),
    ("mm1", 3,), ("opair", 5,), ("mm0", 0,), ("ofw1", 1,), ("opair", 7,), ("ostart", 6,),
    ("ofw0", 7,), ("ofw1", 2,), ("yst", 3,), ("ofw0", 5,), ("ofw1", 5,), ("mm0", 1,),
    ("mm1", 0,), ("ostart", 4,), ("yst", 0,), ("ofw1", 7,), ("ofw0", 6,), ("mm0", 2,),
    ("ym1", 3,), ("ym0", 3,), ("mm0", 5,), ("mm1", 2,), ("ofw0", 4,), ("ym0", 0,),
    ("mm1", 1,), ("yst", 2,), ("mm0", 7,), ("opair", 4,), ("yst", 1,), ("ym1", 0,),
    ("ym2", 3,), ("mm1", 5,), ("ofw1", 4,), ("ym2", 0,), ("yf", 0, 0,), ("opair", 6,),
    ("ofw1", 6,), ("yst", 5,), ("mm1", 7,), ("yst", 7,), ("yf", 0, 3,), ("yf", 0, 1,),
    ("yf", 3, 0,), ("mm0", 4,), ("mm0", 6,), ("ym1", 1,), ("ym0", 1,), ("mm1", 6,),
    ("ym0", 2,), ("yf", 2, 0,), ("mm1", 4,), ("yf", 3, 3,), ("yf", 0, 2,), ("yst", 4,),
    ("yf", 1, 1,), ("yst", 6,), ("yf", 2, 1,), ("ym2", 1,), ("yf", 1, 2,), ("ym0", 7,),
    ("ym0", 5,), ("ym1", 5,), ("yf", 3, 2,), ("ym0", 4,), ("yf", 6, 0,), ("ym1", 2,),
    ("ym1", 4,), ("yf", 5, 1,), ("yf", 4, 0,), ("yf", 7, 0,), ("yf", 1, 3,), ("ym1", 7,),
    ("ym2", 7,), ("ym0", 6,), ("yf", 5, 0,), ("yf", 2, 2,), ("yf", 3, 1,), ("yf", 1, 0,),
    ("ym2", 2,), ("ym2", 4,), ("yf", 4, 1,), ("yf", 7, 3,), ("ye", 0,), ("yf", 7, 1,),
    ("ym1", 6,), ("yf", 4, 2,), ("ym2", 5,), ("ym2", 6,), ("yf", 6, 1,), ("yf", 2, 3,),
    ("yf", 5, 2,), ("yf", 7, 2,), ("yf", 4, 3,), ("yf", 6, 2,), ("ye", 1,), ("yf", 5, 3,),
    ("yf", 6, 3,), ("ye", 3,), ("ye", 5,), ("ye", 7,), ("ye", 2,), ("ye", 4,),
    ("ye", 6,),
)
HL = L // 2
SCALE = (HD ** -0.5) * 1.4426950408889634
U = 16
DR = L - 8 * U
BF = jnp.bfloat16
F32 = jnp.float32


def mod(a, n):
    return lax.rem(a + n, n)


def kernel(x_hbm, seg_hbm, wq_hbm, wk_hbm, wv_hbm, wo_hbm, yg,
           xbuf, wbuf, acc, kloc, vloc, qloc, kg, vg, qg, obuf, og, wt, psend, pown, rsb, segs, sk, m_s, l_s, o_s,
           x_sem, w_sem, wo_sem, ws_send, ws_recv, wf_send, wf_recv, sh_send, sh_recv, wx_send, wx_recv,
           kv_send, kv_recv, kf_send, kf_recv, q_send, q_recv, o_send, o_recv,
           sg_send, sg_recv, sg_loc, a_send, a_recv, r_send, r_recv, y_send, y_recv):
    t = lax.axis_index("tp")
    c = lax.axis_index("cp")
    x, k = c // 2, lax.rem(c, 2)
    z, y = t // NX, lax.rem(t, NX)
    yh, yb = y // 2, lax.rem(y, 2)
    xodd = lax.rem(x, 2)
    partner = {"cp": x * 2 + 1 - k}

    def iy(yy):
        return lax.rem(yy + yy // 2, 2)

    def slice_of(zz, yy):
        return zz * 2 + iy(yy)

    def piece_of(zz, yy):
        return slice_of(zz, yy) * 2 + yy // 2

    def tpdev(zz, yy):
        return {"tp": zz * NX + yy}

    def rcopy(src, dst, ss, rs, dev):
        return pltpu.make_async_remote_copy(src_ref=src, dst_ref=dst, send_sem=ss, recv_sem=rs, device_id=dev, device_id_type=MESH)

    s_me = z * 2 + yb
    sl_me = slice_of(z, y)
    sends = []

    def x_copy(i):
        return pltpu.make_async_copy(x_hbm.at[:, pl.ds(pl.multiple_of(i * KC, KC), KC)], xbuf.at[i], x_sem.at[i])

    w_hbms = (wk_hbm, wv_hbm, wq_hbm)

    def w_copies(w, i):
        g = lax.rem(4 * w + i, 3) * 2
        return [pltpu.make_async_copy(w_hbms[w].at[pl.ds(pl.multiple_of((2 * i + b) * KC, KC), KC), :], wbuf.at[g + b], w_sem.at[g + b]) for b in range(2)]

    def load(w, i):
        for b, cp_ in enumerate(w_copies(w, i)):
            if w == 0:
                x_copy(2 * i + b).start()
            cp_.start()

    for i in range(2):
        load(0, jnp.int32(i))
    seg_own = pltpu.make_async_copy(seg_hbm, segs.at[c], sg_loc)
    seg_own.start()
    my_cols = pl.ds(pl.multiple_of(sl_me * 1024, 1024), 1024)

    def share(cc):
        return pl.ds(pl.multiple_of(DR + cc * U, U), U)

    wo_own = [pltpu.make_async_copy(wo_hbm.at[pl.ds(0, DR), my_cols], wt.at[s_me, pl.ds(0, DR), :], wo_sem.at[0]),
              pltpu.make_async_copy(wo_hbm.at[share(c), my_cols], wt.at[s_me, share(c), :], wo_sem.at[1])]

    bar = pltpu.get_barrier_semaphore()
    n_peers = 0
    for dc in range(1, 2 * NX):
        pl.semaphore_signal(bar, inc=1, device_id={"cp": mod(c + dc, 2 * NX)}, device_id_type=MESH)
        n_peers += 1
    for dz in range(NX):
        for e in range(2):
            if dz or e:
                pl.semaphore_signal(bar, inc=1, device_id=tpdev(mod(z + dz, NX), yh * 2 + lax.rem(yb + e, 2)), device_id_type=MESH)
                n_peers += 1
    pl.semaphore_signal(bar, inc=1, device_id=tpdev(z, 3 - y), device_id_type=MESH)
    n_peers += 1

    HR = DR // 2

    def w_move(dz, e, shared):
        z2, y2 = mod(z + dz, NX), yh * 2 + lax.rem(yb + e, 2)
        i = dz * 2 + e - 1
        rows = share(c) if shared else pl.ds(pl.multiple_of(k * HR, HR), HR)
        return rcopy(wo_hbm.at[rows, pl.ds(pl.multiple_of(slice_of(z2, y2) * 1024, 1024), 1024)], wt.at[s_me, rows, :],
                     sh_send.at[i] if shared else ws_send.at[i], sh_recv.at[i] if shared else ws_recv.at[i], tpdev(z2, y2))

    def w_slot(dz, e):
        return mod(z - dz, NX) * 2 + lax.rem(yb + e, 2)

    def w_rows(dz, e, kk):
        return wt.at[w_slot(dz, e), pl.ds(pl.multiple_of(kk * HR, HR), HR), :]

    def w_fwd(dz, e, kk):
        i = dz * 2 + e - 1
        ref = w_rows(dz, e, kk)
        return rcopy(ref, ref, wf_send.at[i], wf_recv.at[i], partner)

    def wx(idx, cc, half, dev):
        cols = pl.ds(0, 1024) if half is None else pl.ds(half * 512, 512)
        ref = wt.at[:, share(cc), cols]
        return rcopy(ref, ref, wx_send.at[idx], wx_recv.at[idx], dev)

    def xdev(dx):
        return {"cp": mod(x + dx, NX) * 2 + k}

    def blk(dx, kk):
        return mod(x + dx, NX) * 2 + kk

    def go(cp_):
        cp_.start()
        sends.append(cp_)

    def wx_start():
        for dz, e in group:
            i = dz * 2 + e - 1
            ref = wt.at[w_slot(dz, e), share(c), :]
            rcopy(ref, ref, sh_send.at[i], sh_recv.at[i], partner).wait_recv()
        wo_own[1].wait()
        go(wx(0, c, 0, xdev(1)))
        go(wx(1, c, 1, xdev(3)))
        go(wx(2, c, None, partner))

    def wx_second():
        go(wx(8, c, 1, xdev(1)))
        go(wx(9, c, 0, xdev(3)))

    def wx_relay():
        wx(0, blk(3, k), 0, partner).wait_recv()
        go(wx(3, blk(3, k), 0, xdev(1)))
        wx(1, blk(1, k), 1, partner).wait_recv()
        go(wx(5, blk(1, k), 1, xdev(3)))

    def wx_last():
        w_forward()
        wx(8, blk(3, k), 1, partner).wait_recv()
        go(wx(4, blk(3, k), None, partner))
        wx(9, blk(1, k), 0, partner).wait_recv()
        go(wx(6, blk(1, k), None, partner))
        wx(3, blk(2, k), 0, partner).wait_recv()
        wx(5, blk(2, k), 1, partner).wait_recv()
        go(wx(7, blk(2, k), None, partner))

    def w_forward():
        for dz, e in group:
            i = dz * 2 + e - 1
            ref = w_rows(dz, e, k)
            rcopy(ref, ref, ws_send.at[i], ws_recv.at[i], partner).wait_recv()
            go(w_fwd(dz, e, k))

    def w_done():
        wo_own[0].wait()
        for dz, e in group:
            w_fwd(dz, e, 1 - k).wait_recv()
        wx(2, blk(0, 1 - k), None, partner).wait_recv()
        wx(4, blk(3, 1 - k), None, partner).wait_recv()
        wx(6, blk(1, 1 - k), None, partner).wait_recv()
        wx(7, blk(2, 1 - k), None, partner).wait_recv()

    group = [(dz, e) for dz in range(NX) for e in range(2) if dz or e]
    def spread_w():
        pl.semaphore_wait(bar, n_peers)
        seg_own.wait()
        for dc in range(1, 2 * NX):
            cp_ = rcopy(segs.at[c], segs.at[c], sg_send.at[dc - 1], sg_recv.at[dc - 1], {"cp": mod(c + dc, 2 * NX)})
            cp_.start()
            sends.append(cp_)
        for shared in (True, False):
            for dz, e in group:
                go(w_move(dz, e, shared))
        for cp_ in reversed(wo_own):
            cp_.start()

    def project(w, lo, hi):
        def step(i, _):
            nxt = i + 2

            @pl.when(nxt < NKC // 2)
            def _():
                load(w, nxt)
            if w < 2:
                @pl.when(nxt >= NKC // 2)
                def _():
                    load(w + 1, nxt - NKC // 2)
            for b, cp_ in enumerate(w_copies(w, i)):
                cp_.wait()
                if w == 0:
                    x_copy(2 * i + b).wait()
            g = lax.rem(4 * w + i, 3) * 2
            acc[...] += (jnp.dot(xbuf[2 * i], wbuf[g], preferred_element_type=F32)
                         + jnp.dot(xbuf[2 * i + 1], wbuf[g + 1], preferred_element_type=F32))
            return 0
        lax.fori_loop(lo, hi, step, 0)

    def split(dst):
        for h in range(4):
            dst[h] = acc[:, h * HD:(h + 1) * HD].astype(BF)

    def kv_copy(n, idx, src, dst, dev):
        return rcopy(src, dst, kv_send.at[n, idx], kv_recv.at[n, idx], dev)

    def kv_spread(n, loc, gat):
        for dx in (2, 1, 3):
            go(kv_copy(n, dx - 1, loc.at[mod(x + dx, NX)], gat.at[c], xdev(dx)))
        go(kv_copy(n, 3, loc.at[x], gat.at[c], partner))
        gat[c] = loc[x]

    def kv_forward(n, gat):
        for dx in (1, 3, 2):
            ref = gat.at[blk(4 - dx, k)]
            kv_copy(n, dx - 1, ref, ref, partner).wait_recv()
            go(rcopy(ref, ref, kf_send.at[n, dx - 1], kf_recv.at[n, dx - 1], partner))

    def kv_finish(n, gat):
        ref = gat.at[blk(0, 1 - k)]
        kv_copy(n, 3, ref, ref, partner).wait_recv()
        for dx in (1, 3, 2):
            ref = gat.at[blk(4 - dx, 1 - k)]
            rcopy(ref, ref, kf_send.at[n, dx - 1], kf_recv.at[n, dx - 1], partner).wait_recv()

    acc[...] = jnp.zeros_like(acc)
    with jax.named_scope("proj_k0"):
        project(0, 0, 2)
    with jax.named_scope("barrier"):
        spread_w()
    with jax.named_scope("proj_k1"):
        project(0, 2, 4)
    split(kloc)
    acc[...] = jnp.zeros_like(acc)
    kv_spread(0, kloc, kg)
    with jax.named_scope("proj_v"):
        project(1, 0, 4)
    for h in range(4):
        vloc[h] = jnp.transpose(acc[:, h * HD:(h + 1) * HD]).astype(BF)
    acc[...] = jnp.zeros_like(acc)
    kv_spread(1, vloc, vg)
    with jax.named_scope("proj_q0"):
        project(2, 0, 2)
    with jax.named_scope("fwd_k"):
        kv_forward(0, kg)
    with jax.named_scope("proj_q1"):
        project(2, 2, 4)
    split(qloc)
    own = lax.rem(x + k, 2)
    for dx in (2, 1, 3):
        h = mod(x + dx, NX)
        cp_ = rcopy(qloc.at[h], qg.at[x], q_send.at[dx - 1], q_recv.at[x], {"cp": h * 2 + own})
        cp_.start()
        sends.append(cp_)

    @pl.when(xodd == 0)
    def _():
        qg[x] = qloc[x]

    q_d2d = rcopy(qloc.at[x], qg.at[x], q_send.at[3], q_recv.at[x], partner)

    @pl.when(xodd == 1)
    def _():
        q_d2d.start()

    with jax.named_scope("segs"):
        for dc in range(1, 2 * NX):
            ref = segs.at[mod(c - dc, 2 * NX)]
            rcopy(ref, ref, sg_send.at[dc - 1], sg_recv.at[dc - 1], partner).wait_recv()

        def seg_columns(j, _):
            sk[j] = jnp.transpose(jnp.broadcast_to(segs[j], (HD, L)))
            return 0
        lax.fori_loop(0, 2 * NX, seg_columns, 0)
    with jax.named_scope("fwd_v"):
        kv_forward(1, vg)

    with jax.named_scope("fin_kv"):
        kv_finish(0, kg)
        kv_finish(1, vg)
    tiles = [slice(b, b + HL) for b in range(0, L, HL)]

    def q_block(xx):
        return 2 * xx + lax.rem(k + xx, 2)

    def local(xx):
        return (x == xx) & (xodd == 0)

    def scores(xx, j, n, rows, diag):
        s = lax.dot_general(kg[j, 0:n, :], qg[xx, rows, :], (((1,), (1,)), ((), ())), preferred_element_type=F32)
        ok = jnp.concatenate([sk[j, 0:n, :]] * (HL // HD), axis=1) == jnp.broadcast_to(segs[q_block(xx)][:, rows], (n, HL))
        if diag:
            qi = lax.broadcasted_iota(jnp.int32, (n, HL), 1) + rows.start
            ok = ok & (lax.broadcasted_iota(jnp.int32, (n, HL), 0) <= qi)
        return jnp.where(ok, s * SCALE, -jnp.inf)

    def update(xx, blocks):
        for rows in tiles:
            ss = [scores(xx, j, L, rows, False) for j in blocks]
            m = m_s[xx, :, rows]
            m_new = m
            for s in ss:
                m_new = jnp.maximum(m_new, jnp.max(s, axis=0, keepdims=True))
            alpha = jnp.exp2(m - m_new)
            l, o = l_s[xx, :, rows] * alpha, o_s[xx, :, rows] * alpha
            for j, s in zip(blocks, ss):
                p = jnp.exp2(s - m_new)
                l += jnp.sum(p, axis=0, keepdims=True)
                o += jnp.dot(vg[j], p.astype(BF), preferred_element_type=F32)
            m_s[xx, :, rows], l_s[xx, :, rows], o_s[xx, :, rows] = m_new, l, o

    def o_ret(xx):
        ocol = pl.ds(pl.multiple_of(s_me * F + x * HD, HD), HD)
        return rcopy(obuf.at[xx], og.at[:, ocol], o_send.at[xx], o_recv.at[x], {"cp": q_block(xx)}), ocol

    def finish(xx):
        obuf[xx] = jnp.transpose(o_s[xx] / l_s[xx]).astype(BF)
        ret, ocol = o_ret(xx)

        @pl.when(local(xx))
        def _():
            og[:, ocol] = obuf[xx]

        pl.when(jnp.logical_not(local(xx)))(ret.start)

    def attend_own():
        for xx in range(NX):
            c_q = q_block(xx)
            for rows in tiles:
                s = scores(xx, c_q, rows.stop, rows, True)
                m = jnp.max(s, axis=0, keepdims=True)
                p = jnp.exp2(s - m)
                m_s[xx, :, rows] = m
                l_s[xx, :, rows] = jnp.sum(p, axis=0, keepdims=True)
                o_s[xx, :, rows] = jnp.dot(vg[c_q, :, 0:rows.stop], p.astype(BF), preferred_element_type=F32)
        for xx in (1 - k, 3 - k):
            update(xx, [2 * xx])
        finish(0)

    def attend_chip(i):
        for n in range(NX - 1 - i):
            xx = n + i + 1 if i else 1 + lax.rem(x + n, NX - 1)
            update(xx, [2 * i, 2 * i + 1])
            if i == 0:
                finish(xx)

    def wait_o():
        for h in range(NX):
            o_in = rcopy(obuf.at[0], og.at[:, pl.ds(pl.multiple_of(s_me * F + h * HD, HD), HD)], o_send.at[0], o_recv.at[h], partner)
            pl.when(jnp.logical_not((x == h) & (xodd == 0)))(o_in.wait_recv)

    with jax.named_scope("wait_q"):
        for xx in range(NX):
            pl.when(jnp.logical_not(local(xx)))(rcopy(qg.at[xx], qg.at[xx], q_send.at[3], q_recv.at[xx], partner).wait_recv)
    with jax.named_scope("wx_start"):
        wx_start()
    with jax.named_scope("attn"):
        attend_own()
    wx_second()
    with jax.named_scope("attn2"):
        attend_chip(2)
    with jax.named_scope("attn1"):
        attend_chip(1)
    with jax.named_scope("wx_relay"):
        wx_relay()
    with jax.named_scope("attn0"):
        attend_chip(0)

    def row_ds(r):
        return pl.ds(ROWS[r][0], ROWS[r][1])

    def o_copy(r, idx, zz, e, dev):
        s = zz * 2 + lax.rem(yb + e, 2)
        ref = og.at[row_ds(r), pl.ds(pl.multiple_of(s * F, F), F)]
        return rcopy(ref, ref, a_send.at[r, idx], a_recv.at[r, idx], dev)

    def o_send_z(r, e):
        d = O_DIR[r]
        go(o_copy(r, 1 + 3 * e, z, e, tpdev(mod(z + d, NX), y)))
        go(o_copy(r, 2 + 3 * e, z, e, tpdev(mod(z + NX - d, NX), y)))

    pair = tpdev(z, yh * 2 + 1 - yb)
    o_seen = []

    def ostart(r):
        if not o_seen:
            o_seen.append(r)
            with jax.named_scope("wait_o"):
                wait_o()
        go(o_copy(r, 0, z, 0, pair))
        o_send_z(r, 0)
        if len(o_seen) == 1:
            o_seen.append(r)

    def o_forward(r, e):
        d = O_DIR[r]
        zz = mod(z + NX - d, NX)
        o_copy(r, 1 + 3 * e, zz, e, partner).wait_recv()
        go(o_copy(r, 3 + 3 * e, zz, e, tpdev(mod(z + d, NX), y)))

    def o_pair(r, idx, new, zz):
        o_copy(r, idx, zz, 0, partner).wait_recv()
        go(o_copy(r, new, zz, 0, pair))

    def opair(r):
        if O_FIRST[r] == 0:
            o_pair(r, 2, 5, mod(z + O_DIR[r], NX))
            return
        o_copy(r, 0, z, 1, partner).wait_recv()
        o_send_z(r, 1)

    def ofw0(r):
        o_forward(r, 0)
        if O_FIRST[r] == 0:
            go(o_copy(r, 4, mod(z + NX - O_DIR[r], NX), 0, pair))

    def ofw1(r):
        if O_FIRST[r] == 0:
            o_pair(r, 3, 6, mod(z + 2, NX))
            return
        o_forward(r, 1)

    def o_rest(r):
        d = O_DIR[r]
        if O_FIRST[r] == 0:
            for idx, zz in ((0, z), (4, mod(z + NX - d, NX)), (5, mod(z + d, NX)), (6, mod(z + 2, NX))):
                o_copy(r, idx, zz, 1, partner).wait_recv()
            return
        for e in range(2):
            o_copy(r, 2 + 3 * e, mod(z + d, NX), e, partner).wait_recv()
            o_copy(r, 3 + 3 * e, mod(z + 2, NX), e, partner).wait_recv()

    def matmul(r, half):
        out = psend if half == 0 else pown
        hh = (1 - yh) if half == 0 else yh
        a, n = ROWS[r]
        for b in range(2):
            cols = pl.ds(pl.multiple_of(hh * F + b * 256, 256), 256)
            out[a:a + n, b * 256:(b + 1) * 256] = jnp.dot(og[a:a + n, :], wt[:, :, cols].reshape(8 * F, 256), preferred_element_type=F32)

    def rs_copy(r):
        return rcopy(psend.at[row_ds(r), :], rsb.at[row_ds(r), :], r_send.at[r], r_recv.at[r], tpdev(z, 3 - y))

    def mm0(r):
        o_rest(r)
        if r == first_mm:
            with jax.named_scope("w_done"):
                w_done()
        matmul(r, 0)
        go(rs_copy(r))

    def y_pos(r, a, b):
        if Y_ORDER[r] == 0:
            return mod(z + a, NX), mod(y + b, NX)
        return mod(z + b, NX), mod(y + a, NX)

    def y_ref(r, pos):
        return yg.at[row_ds(r), pl.ds(pl.multiple_of(piece_of(*pos) * F, F), F)]

    def y_copy(r, idx, pos, dev):
        ref = y_ref(r, pos)
        return rcopy(ref, ref, y_send.at[r, idx], y_recv.at[r, idx], dev)

    def y_second(r, j, a):
        d2 = Y_DIR[r][1]
        pos = y_pos(r, a, 0)
        go(y_copy(r, 3 + 3 * j, pos, tpdev(*y_pos(r, 0, d2))))
        go(y_copy(r, 4 + 3 * j, pos, tpdev(*y_pos(r, 0, NX - d2))))

    def yst(r):
        rs_copy(r).wait_recv()
        a, n = ROWS[r]
        yg[a:a + n, pl.ds(pl.multiple_of(piece_of(z, y) * F, F), F)] = (pown[a:a + n, :] + rsb[a:a + n, :]).astype(BF)
        d = Y_DIR[r][0]
        pos = y_pos(r, 0, 0)
        go(y_copy(r, 0, pos, tpdev(*y_pos(r, d, 0))))
        go(y_copy(r, 1, pos, tpdev(*y_pos(r, NX - d, 0))))
        y_second(r, 0, 0)

    def ym0(r):
        d = Y_DIR[r][0]
        pos = y_pos(r, NX - d, 0)
        y_copy(r, 0, pos, partner).wait_recv()
        go(y_copy(r, 2, pos, tpdev(*y_pos(r, d, 0))))
        y_second(r, 1, NX - d)

    def ym1(r):
        d = Y_DIR[r][0]
        y_copy(r, 1, y_pos(r, d, 0), partner).wait_recv()
        y_second(r, 2, d)

    def ym2(r):
        y_copy(r, 2, y_pos(r, 2, 0), partner).wait_recv()
        y_second(r, 3, 2)

    def y_offs(r):
        d = Y_DIR[r][0]
        return (0, NX - d, d, 2)

    def yf(r, j):
        d2 = Y_DIR[r][1]
        pos = y_pos(r, y_offs(r)[j], NX - d2)
        y_copy(r, 3 + 3 * j, pos, partner).wait_recv()
        go(y_copy(r, 5 + 3 * j, pos, tpdev(*y_pos(r, 0, d2))))

    def ye(r):
        d2 = Y_DIR[r][1]
        for j, a in enumerate(y_offs(r)):
            y_copy(r, 4 + 3 * j, y_pos(r, a, d2), partner).wait_recv()
            y_copy(r, 5 + 3 * j, y_pos(r, a, 2), partner).wait_recv()

    steps = dict(ostart=ostart, opair=opair, ofw0=ofw0, ofw1=ofw1, mm0=mm0,
                 mm1=lambda r: matmul(r, 1), wxl=wx_last, yst=yst, ym0=ym0, ym1=ym1, ym2=ym2, yf=yf, ye=ye)
    first_mm = [a[1] for a in ORDER if a[0] == "mm0"][0]
    for name, *args in ORDER:
        with jax.named_scope(name + "_".join(str(a) for a in args)):
            steps[name](*args)

    for cp_ in sends:
        cp_.wait_send()

    @pl.when(xodd == 1)
    def _():
        q_d2d.wait_send()

    for xx in range(NX):
        pl.when(jnp.logical_not(local(xx)))(o_ret(xx)[0].wait_send)


def solution(mesh):
    def body(x, doc, wq, wk, wv, wo):
        seg = doc.reshape(1, L)
        dma = pltpu.SemaphoreType.DMA
        any_ = pl.BlockSpec(memory_space=pl.ANY)
        return pl.pallas_call(
            kernel,
            out_shape=pltpu.VMEM((L, D), BF),
            in_specs=[any_] * 6,
            out_specs=pl.BlockSpec(memory_space=pltpu.VMEM),
            scratch_shapes=[
                pltpu.VMEM((NKC, L, KC), BF), pltpu.VMEM((NB, KC, F), BF), pltpu.VMEM((L, F), F32),
                pltpu.VMEM((4, L, HD), BF), pltpu.VMEM((4, HD, L), BF), pltpu.VMEM((4, L, HD), BF),
                pltpu.VMEM((8, L, HD), BF), pltpu.VMEM((8, HD, L), BF), pltpu.VMEM((4, L, HD), BF), pltpu.VMEM((4, L, HD), BF),
                pltpu.VMEM((L, 8 * F), BF), pltpu.VMEM((8, F, 1024), BF),
                pltpu.VMEM((L, F), F32), pltpu.VMEM((L, F), F32), pltpu.VMEM((L, F), F32),
                pltpu.VMEM((8, 1, L), jnp.int32), pltpu.VMEM((8, L, HD), jnp.int32),
                pltpu.VMEM((NX, 1, L), F32), pltpu.VMEM((NX, 1, L), F32), pltpu.VMEM((NX, HD, L), F32),
                dma((NKC,)), dma((NB,)), dma((2,)), dma((7,)), dma((7,)), dma((7,)), dma((7,)), dma((7,)), dma((7,)), dma((10,)), dma((10,)),
                dma((2, 4)), dma((2, 4)), dma((2, 3)), dma((2, 3)), dma((4,)), dma((4,)), dma((4,)), dma((4,)),
                dma((7,)), dma((7,)), dma, dma((R, 7)), dma((R, 7)), dma((R,)), dma((R,)), dma((R, 15)), dma((R, 15)),
            ],
            compiler_params=pltpu.CompilerParams(collective_id=0, has_side_effects=True, vmem_limit_bytes=50 * 1024 * 1024),
        )(x, seg, wq, wk, wv, wo)

    return jax.shard_map(body, mesh=mesh, in_specs=(P(('dp', 'cp'), None), P(('dp', 'cp')), P(None, 'tp'), P(None, 'tp'), P(None, 'tp'), P('tp', None)), out_specs=P(('dp', 'cp'), None), check_vma=False)
```

time: 142 us -> 134 us (0.944); the launches traced: 142 us -> 132 us
  Pallas kernels: 139 us -> 129 us
    pallas_call x1, Pallas kernels: 139 us -> 129 us  [body(): pl.pallas_call(kernel, out_shape=pltpu.VMEM((L, D), BF), in_specs=[any_]...]
where the time goes in v3:
time: 134 us; the launch traced here: 132 us
  Pallas kernels  129 us (96%)
  local copies, waits for them, and re-layouts  3.4 us (3%)
    pallas_call x1, Pallas kernels, body(): pl.pallas_call(kernel, out_shape=pltpu.VMEM((L, D), BF), in_specs=[any_]...  129 us
    unnamed x1, local copies, waits for them, and re-layouts  3.4 us

profile of v3, /device:TPU:2, one launch (start us, length us, event | category | flops | bytes accessed | tf_op | source)
XLA Modules:
  0.0 132.5 jit_solution(9020122550175625236)
XLA Ops:
  0.0 129.0 %shard_map.64 = bf16[512,8192]{1,0:T(8,128)(2,1)S(1)} custom-call(bf16[512,8192]{1,0:T(8,128)(2,1)} %x_hbm.1, s32[1,512]{1,0:T(1,128)} %bitcast.1, bf16[8192,512]{1,0:T(8,128)(2,1)} %wq_hbm.1, bf16[8192,512]{1,0:T(8,128)(2,1)} %wk_hbm.1, bf16[8192,512]{1,0:T(8,128)(2,1)} %wv_hbm.1, bf16[512,8192]{1,0:T(8,128)(2,1)} %wo_hbm.1), custom_call_target="tpu_custom_call" | custom-call | tf_op jit(solution)/shard_map/pallas_call | solution.py:581
  129.1 3.4 %copy.8 = bf16[512,8192]{1,0:T(8,128)(2,1)} copy(bf16[512,8192]{1,0:T(8,128)(2,1)S(1)} %shard_map.64) | data formatting | bytes 16777216
